TPU v7x, 32 devices: a whole 2x2x4 slice. The times are simulated.
32 devices in a mesh: dp: 4 (over z), ep: 8 (over y, x, core).
Axes of the slice: x: 2, y: 2, z: 4, core: 2. Of those that a mesh axis runs over, the one named last changes fastest.
Arguments:
- hidden: bfloat16 [4096, 4096], P(('dp', 'ep')), parts along dimension 0
- k_cache: bfloat16 [4096, 32, 8, 128], P(('dp', 'ep')), parts along dimension 0
- v_cache: bfloat16 [4096, 32, 8, 128], P(('dp', 'ep')), parts along dimension 0
- seq_lens: int32 [4096], P(('dp', 'ep')), parts along dimension 0
- expert_ids: int32 [4096, 2], P(('dp', 'ep')), parts along dimension 0
- attn_gain: bfloat16 [4096], replicated
- w_query: bfloat16 [4096, 4096], replicated
- w_key: bfloat16 [4096, 1024], replicated
- w_value: bfloat16 [4096, 1024], replicated
- w_out: bfloat16 [4096, 4096], replicated
- ffn_gain: bfloat16 [4096], replicated
- w_router: bfloat16 [4096, 16], replicated
- w_gate: bfloat16 [16, 4096, 960], P('ep')
- w_up: bfloat16 [16, 4096, 960], P('ep')
- w_down: bfloat16 [16, 960, 4096], P('ep')
Outputs:
- output 1: bfloat16 [4096, 4096], P(('dp', 'ep')), parts along dimension 0
- output 2: bfloat16 [4096, 32, 8, 128], P(('dp', 'ep')), parts along dimension 0
- output 3: bfloat16 [4096, 32, 8, 128], P(('dp', 'ep')), parts along dimension 0
There are 4 independent parts. A program takes and returns all parts, laid end to end along the dimension named above; an argument that names none is the same for every part.
All inputs are finite; a program needn't handle non-finite values.
Results may differ from a plain program's by a relative error of at most 0.0149365.
Values are sent between devices in bfloat16 or wider.
A program may use at most 1 GiB of HBM per device.

v0:
```python
import jax
import jax.numpy as jnp
from jax import lax
from jax.sharding import PartitionSpec as P

NORM_EPS = 1e-5
ROPE_THETA = 1000000.0


def rms_scale(row_block, gain_vec):
    rows_f32 = row_block.astype(jnp.float32)
    inv_rms = lax.rsqrt(jnp.mean(rows_f32 * rows_f32, axis=-1, keepdims=True) + NORM_EPS)
    return (rows_f32 * inv_rms * gain_vec.astype(jnp.float32)).astype(jnp.bfloat16)


def rope_rotate(vectors, positions):
    half_dim = vectors.shape[-1] // 2
    inv_freq = ROPE_THETA ** (-2.0 * jnp.arange(half_dim, dtype=jnp.float32) / vectors.shape[-1])
    angles = positions.astype(jnp.float32)[:, None, None] * inv_freq
    cosines = jnp.cos(angles)
    sine_vals = jnp.sin(angles)
    vec_f32 = vectors.astype(jnp.float32)
    low_half = vec_f32[..., :half_dim]
    high_half = vec_f32[..., half_dim:]
    return jnp.concatenate([low_half * cosines - high_half * sine_vals, high_half * cosines + low_half * sine_vals], axis=-1).astype(jnp.bfloat16)


def attention_block(hidden, k_cache, v_cache, seq_lens, attn_gain, w_query, w_key, w_value, w_out):
    tokens, seq_len, kv_heads, head_dim = k_cache.shape
    q_heads = w_query.shape[1] // head_dim
    groups = q_heads // kv_heads
    normed = rms_scale(hidden, attn_gain)
    q_proj = jnp.dot(normed, w_query, preferred_element_type=jnp.float32).astype(jnp.bfloat16)
    q_proj = rope_rotate(q_proj.reshape(tokens, q_heads, head_dim), seq_lens).reshape(tokens, kv_heads, groups, head_dim)
    key_new = jnp.dot(normed, w_key, preferred_element_type=jnp.float32).astype(jnp.bfloat16)
    key_new = rope_rotate(key_new.reshape(tokens, kv_heads, head_dim), seq_lens)
    value_new = jnp.dot(normed, w_value, preferred_element_type=jnp.float32).astype(jnp.bfloat16).reshape(tokens, kv_heads, head_dim)
    positions = jnp.arange(seq_len)
    slot_hit = (positions[None, :] == seq_lens[:, None])[:, :, None, None]
    k_cache_new = jnp.where(slot_hit, key_new[:, None], k_cache)
    v_cache_new = jnp.where(slot_hit, value_new[:, None], v_cache)
    scores = jnp.einsum('tkgh,tskh->tkgs', q_proj, k_cache_new, preferred_element_type=jnp.float32) * head_dim ** -0.5
    visible = (positions[None, :] <= seq_lens[:, None])[:, None, None, :]
    attn_probs = jax.nn.softmax(jnp.where(visible, scores, -jnp.inf), axis=-1).astype(jnp.bfloat16)
    attn_mix = jnp.einsum('tkgs,tskh->tkgh', attn_probs, v_cache_new, preferred_element_type=jnp.float32).astype(jnp.bfloat16)
    attn_out = jnp.dot(attn_mix.reshape(tokens, q_heads * head_dim), w_out, preferred_element_type=jnp.float32)
    resid_out = (hidden.astype(jnp.float32) + attn_out).astype(jnp.bfloat16)
    return resid_out, k_cache_new, v_cache_new


def ffn_gates(resid_out, ffn_gain, w_router, expert_ids):
    normed_ffn = rms_scale(resid_out, ffn_gain)
    logits = jnp.dot(normed_ffn, w_router, preferred_element_type=jnp.float32)
    chosen = expert_ids[:, :, None] == jnp.arange(w_router.shape[1])
    picked = jnp.sum(jnp.where(chosen, logits[:, None, :], 0.0), axis=-1)
    return normed_ffn, jax.nn.softmax(picked, axis=-1)


def choice_slots(expert_ids, expert_list, cap_slots):
    hit_mask = expert_ids[..., None] == expert_list
    hit_counts = hit_mask.reshape(hit_mask.shape[:-3] + (-1, hit_mask.shape[-1])).astype(jnp.int32)
    before = (jnp.cumsum(hit_counts, axis=-2) - hit_counts).reshape(hit_mask.shape)
    return (hit_mask[..., None] & (before[..., None] == jnp.arange(cap_slots))).astype(jnp.bfloat16)


def solution(mesh):
    n_ep = mesh.shape['ep']
    row_spec = P(('dp', 'ep'), None)
    cache_spec = P(('dp', 'ep'), None, None, None)
    expert_spec = P('ep', None, None)
    in_specs = (row_spec, cache_spec, cache_spec, P(('dp', 'ep')), row_spec, P(), P(), P(), P(), P(), P(), P(), expert_spec, expert_spec, expert_spec)
    out_specs = (row_spec, cache_spec, cache_spec)

    def device_step(hidden, k_cache, v_cache, seq_lens, expert_ids, attn_gain, w_query, w_key, w_value, w_out, ffn_gain, w_router, w_gate, w_up, w_down):
        tokens, d_model = hidden.shape
        local_experts = w_gate.shape[0]
        n_experts = local_experts * n_ep
        cap_slots = 4 * tokens // n_experts
        resid_out, k_cache_new, v_cache_new = attention_block(hidden, k_cache, v_cache, seq_lens, attn_gain, w_query, w_key, w_value, w_out)
        normed_ffn, gates = ffn_gates(resid_out, ffn_gain, w_router, expert_ids)
        slot_sel = choice_slots(expert_ids, jnp.arange(n_experts), cap_slots)
        send_buf = jnp.einsum('tkec,td->ecd', slot_sel, normed_ffn, preferred_element_type=jnp.float32).astype(jnp.bfloat16)
        send_buf = send_buf.reshape(n_ep, local_experts, cap_slots, d_model)
        recv_buf = lax.all_to_all(send_buf, 'ep', 0, 0, tiled=True)
        gate_act = jnp.einsum('sxcd,xdf->sxcf', recv_buf, w_gate, preferred_element_type=jnp.float32)
        up_act = jnp.einsum('sxcd,xdf->sxcf', recv_buf, w_up, preferred_element_type=jnp.float32)
        inner_act = (jax.nn.silu(gate_act) * up_act).astype(jnp.bfloat16)
        expert_out = jnp.einsum('sxcf,xfd->sxcd', inner_act, w_down, preferred_element_type=jnp.float32).astype(jnp.bfloat16)
        returned = lax.all_to_all(expert_out, 'ep', 0, 0, tiled=True).reshape(n_experts, cap_slots, d_model)
        routed = jnp.einsum('tkec,ecd->tkd', slot_sel, returned, preferred_element_type=jnp.float32)
        out_f32 = resid_out.astype(jnp.float32) + jnp.sum(gates[:, :, None] * routed, axis=1)
        return out_f32.astype(jnp.bfloat16), k_cache_new, v_cache_new

    return jax.shard_map(device_step, mesh=mesh, in_specs=in_specs, out_specs=out_specs, check_vma=False)
```

profile of v0, /device:TPU:0, one launch (start us, length us, event | category | flops | bytes accessed | tf_op | source)
XLA Modules:
  0.0 231.5 jit_solution(11672778542323532880)
XLA Ops:
  0.7 0.7 convert_element_type.95
  1.4 0.7 iota_compare_fusion.2
  2.1 0.7 iota_compare_fusion.5
  2.8 0.8 copy.32
  3.9 1.5 fusion.23
  5.4 0.7 convert_element_type.90
  6.1 0.7 convert_element_type.104
  6.8 0.6 reduce-window.6
  7.9 5.1 %fusion.42 = bf16[16,8,8,128]{3,1,2,0:T(8,128)(2,1)S(1)} fusion(bf16[4096,1024]{1,0:T(8,128)(2,1)} %param.23, bf16[128,4096]{1,0:T(8,128)(2,1)} %param.15, f32[4096]{0:T(1024)S(1)} %convert_element_type.90, f32[128]{0:T(128)S(1)} %add_rsqrt_fusion.1), kind=kOutput, calls=%fused_computation.53 | convolution fusion | flops 1075970048 | bytes 9716224 | tf_op jit(solution)/shard_map/dot_general | solution.py:37
  13.0 4.7 %fusion.41 = f32[16,8,8,128]{3,1,2,0:T(8,128)S(1)} fusion(bf16[4096,1024]{1,0:T(8,128)(2,1)} %param.22, bf16[128,4096]{1,0:T(8,128)(2,1)S(1)} %copy-done.1, f32[4096]{0:T(1024)S(1)} %convert_element_type.90, f32[128]{0:T(128)S(1)} %add_rsqrt_fusion.1), kind=kOutput, calls=%fused_computation.52 | convolution fusion | flops 1076101120 | bytes 9978368 | tf_op jit(solution)/shard_map/dot_general | solution.py:35
  17.8 13.0 %fusion.31 = f32[16,8,32,128]{3,1,2,0:T(8,128)S(1)} fusion(bf16[4096,4096]{1,0:T(8,128)(2,1)} %param.21, bf16[128,4096]{1,0:T(8,128)(2,1)S(1)} %copy-done.1, f32[4096]{0:T(1024)S(1)} %convert_element_type.90, f32[128]{0:T(128)S(1)} %add_rsqrt_fusion.1), kind=kOutput, calls=%fused_computation.46 | convolution fusion | flops 4298113024 | bytes 36717056 | tf_op jit(solution)/shard_map/dot_general | solution.py:33
  30.8 0.4 copy.45
  31.2 0.3 multiply_cosine_fusion
  31.5 0.3 subtract_convert_fusion.1
  31.8 0.9 subtract_convert_fusion
  32.9 11.9 %broadcast_select_fusion.1 = (bf16[128,32,8,128]{3,2,1,0:T(8,128)(2,1)}, bf16[128,32,8,128]{3,2,1,0:T(8,128)(2,1)}) fusion(bf16[128,32,8,128]{3,2,1,0:T(8,128)(2,1)} %param.16, pred[128,32]{1,0:T(8,128)(4,1)S(1)} %get-tuple-element.12, bf16[128,8,128]{2,1,0:T(8,128)(2,1)S(1)} %pad_maximum_fusion, bf16[128,32,8,128]{3,2,1,0:T(8,128)(2,1)} %param.17, ...), kind=kLoop, calls=%fused_computation.12 | loop fusion | flops 8388608 | bytes 34082816 | tf_op jit(solution)/shard_map/jit(_where)/select_n | solution.py:40
  44.7 9.4 %fusion.67 = (f32[128,8,4]{2,1,0:T(8,128)}, f32[128,8,4,32]{3,2,1,0:T(4,128)}) fusion(pred[128,32]{1,0:T(8,128)(4,1)S(1)} %get-tuple-element.11, bf16[128,32,8,128]{3,2,1,0:T(8,128)(2,1)} %get-tuple-element.7, bf16[128,8,4,64]{3,2,1,0:T(4,128)(2,1)S(1)} %bitcast.91, bf16[128,8,4,64]{3,2,1,0:T(4,128)(2,1)S(1)} %bitcast.90), kind=kOutput, calls=%fused_computation.94 | convolution fusion | flops 36175904 | bytes 9981952 | tf_op jit(solution)/shard_map/sub | solution.py:44
  54.1 6.5 %fusion.37 = bf16[128,8,4,128]{3,2,1,0:T(4,128)(2,1)S(1)} fusion(bf16[128,32,8,128]{3,2,1,0:T(8,128)(2,1)} %get-tuple-element.8, f32[128,8,4,32]{3,2,1,0:T(4,128)} %get-tuple-element.14, f32[128,8,4]{2,1,0:T(8,128)} %get-tuple-element.13), kind=kOutput, calls=%fused_computation.48 | convolution fusion | flops 34340864 | bytes 9977856 | tf_op jit(solution)/shard_map/tkgs,tskh->tkgh/dot_general | solution.py:45
  60.7 1.6 reshape.214
  62.3 13.3 %multiply_reduce_fusion = (f32[128]{0:T(128)S(1)}, f32[128,4096]{1,0:T(8,128)S(1)}) fusion(bf16[128,4096]{1,0:T(8,128)(2,1)} %reshape.214, bf16[4096,4096]{1,0:T(8,128)(2,1)} %param.24, bf16[128,4096]{1,0:T(8,128)(2,1)S(1)} %copy-done.1), kind=kOutput, calls=%fused_computation.39 | convolution fusion | flops 4298113024 | bytes 37749248 | tf_op jit(solution)/shard_map/dot_general | solution.py:46
  75.7 1.3 convolution_convert_fusion
  77.1 54.1 %all_to_all.10 = bf16[8,2,32,4096]{3,2,1,0:T(8,128)(2,1)} all-to-all(bf16[8,2,32,4096]{3,2,1,0:T(8,128)(2,1)S(1)} %bitcast.87), channel_id=1, replica_groups=mesh['dp'=4,'ep'=8] {'ep'}, dimensions={0} | all-to-all | bytes 8388608 | tf_op jit(solution)/shard_map/all_to_all | solution.py:84
  131.1 12.6 %fusion.5 = f32[2,8,32,960]{3,2,1,0:T(8,128)} fusion(bf16[2,4096,960]{1,2,0:T(8,128)(2,1)} %param.27, bf16[8,2,32,4096]{3,2,1,0:T(8,128)(2,1)} %all_to_all.10), kind=kOutput, calls=%fused_computation.5 | convolution fusion | flops 4026531840 | bytes 21889024 | tf_op jit(solution)/shard_map/sxcd,xdf->sxcf/dot_general | solution.py:85
  143.7 16.6 %fusion.26 = bf16[8,2,32,960]{3,2,0,1:T(8,128)(2,1)S(1)} fusion(f32[2,8,32,960]{3,2,1,0:T(8,128)} %fusion.5, bf16[2,4096,960]{1,2,0:T(8,128)(2,1)} %param.28, bf16[8,2,32,4096]{3,2,1,0:T(8,128)(2,1)} %all_to_all.10), kind=kOutput, calls=%fused_computation.31 | convolution fusion | flops 4029480960 | bytes 22872064 | tf_op jit(solution)/shard_map/sxcd,xdf->sxcf/dot_general | solution.py:86
  160.3 10.2 %fusion.14 = bf16[8,2,32,4096]{3,2,0,1:T(8,128)(2,1)S(1)} fusion(bf16[8,2,32,960]{3,2,0,1:T(8,128)(2,1)S(1)} %fusion.26, bf16[2,960,4096]{2,1,0:T(8,128)(2,1)} %param.29), kind=kOutput, calls=%fused_computation.15 | convolution fusion | flops 4028628992 | bytes 20905984 | tf_op jit(solution)/shard_map/sxcf,xfd->sxcd/dot_general | solution.py:88
  170.6 2.2 copy.39
  172.8 4.5 %all-to-all-start.1 = ((bf16[8,2,32,4096]{3,2,1,0:T(8,128)(2,1)}), bf16[8,2,32,4096]{3,2,1,0:T(8,128)(2,1)}, u32[]{:S(2)}, u32[]{:S(2)}) async-start(bf16[8,2,32,4096]{3,2,1,0:T(8,128)(2,1)} %copy.39), calls=%async_computation.1 | async-start | bytes 8388608 | tf_op jit(solution)/shard_map/all_to_all | solution.py:89
  177.4 0.4 fusion.63
  177.8 0.2 copy-done.2
  178.1 48.2 %all-to-all-done.1 = bf16[8,2,32,4096]{3,2,1,0:T(8,128)(2,1)} async-done(((bf16[8,2,32,4096]{3,2,1,0:T(8,128)(2,1)}), bf16[8,2,32,4096]{3,2,1,0:T(8,128)(2,1)}, u32[]{:S(2)}, u32[]{:S(2)}) %all-to-all-start.1) | async-done | bytes 4194336 | tf_op jit(solution)/shard_map/all_to_all | solution.py:89
  226.3 3.9 %fusion.30 = f32[128,4096]{1,0:T(8,128)S(1)} fusion(bf16[16,32,4096,1]{2,1,0,3:T(8,128)(2,1)} %bitcast.16, f32[128,2]{0,1:T(2,128)S(1)} %fusion.58, s32[128,2,16]{0,2,1:T(8,128)S(1)} %copy.36, pred[128,2,16]{0,2,1:T(8,128)(4,1)S(1)} %iota_compare_fusion.5), kind=kOutput, calls=%fused_computation.45 | convolution fusion | flops 1075576832 | bytes 6312960 | tf_op jit(solution)/shard_map/tkec,ecd->tkd/dot_general | solution.py:90
  230.2 1.2 add_convert_fusion
  (25 shorter events, 1.3 us)
Async XLA Ops:
  0.6 176.7 %copy-start = (bf16[4096,16]{0,1:T(8,128)(2,1)S(1)}, bf16[4096,16]{0,1:T(8,128)(2,1)}, u32[]{:S(2)}) copy-start(bf16[4096,16]{0,1:T(8,128)(2,1)} %param.26) | copy-start | bytes 393220
  7.9 5.2 %copy-start.1 = (bf16[128,4096]{1,0:T(8,128)(2,1)S(1)}, bf16[128,4096]{1,0:T(8,128)(2,1)}, u32[]{:S(2)}) copy-start(bf16[128,4096]{1,0:T(8,128)(2,1)} %param.15) | copy-start | bytes 3145732
  172.8 53.5 %all-to-all-start.1 = ((bf16[8,2,32,4096]{3,2,1,0:T(8,128)(2,1)}), bf16[8,2,32,4096]{3,2,1,0:T(8,128)(2,1)}, u32[]{:S(2)}, u32[]{:S(2)}) async-start(bf16[8,2,32,4096]{3,2,1,0:T(8,128)(2,1)} %copy.39), calls=%async_computation.1 | async-start | bytes 8388608 | tf_op jit(solution)/shard_map/all_to_all | solution.py:89
  177.4 0.7 copy-start.2
where the time goes:
time: 232 us; the launch traced here: 231 us
  matrix products  97.1 us (42%)
  blocking collectives  54.1 us (23%)
  waiting for transfers between devices  48.2 us (21%)
  other arithmetic  20.7 us (9%)
  local copies, waits for them, and re-layouts  6.01 us (3%)
  starting transfers between devices  4.54 us (2%)
    all_to_all x1, blocking collectives, device_step(): recv_buf = lax.all_to_all(send_buf, 'ep', 0, 0, tiled=True)  54.1 us
    all_to_all x1, waiting for transfers between devices, device_step(): lax.all_to_all(expert_out, 'ep', 0, 0, tiled=True)  48.2 us
    dot_general x1, matrix products, device_step(): jnp.einsum('sxcd,xdf->sxcf', recv_buf, w_up, preferred_element_type=jnp.f...  16.6 us
    dot_general x1, matrix products, attention_block(): jnp.dot(attn_mix.reshape(tokens, q_heads * head_dim), w_out, preferred_el...  13.3 us
    dot_general x1, matrix products, attention_block(): jnp.dot(normed, w_query, preferred_element_type=jnp.float32)  13 us
    dot_general x1, matrix products, device_step(): jnp.einsum('sxcd,xdf->sxcf', recv_buf, w_gate, preferred_element_type=jnp...  12.6 us
    select_n x1, other arithmetic, attention_block(): k_cache_new = jnp.where(slot_hit, key_new[:, None], k_cache)  11.9 us
    dot_general x1, matrix products, device_step(): jnp.einsum('sxcf,xfd->sxcd', inner_act, w_down, preferred_element_type=jn...  10.2 us
  transfers between devices with their start and end apart: 1, of which 1 were waited for; matrix products, arithmetic and copies ran while one was open for 0% of the time, Pallas kernels for 0%

commit v1 on v0

v1 whole, which is shorter than its diff:
```python
import functools

import jax
import jax.numpy as jnp
from jax import lax
from jax.experimental import pallas as pl
from jax.experimental.pallas import tpu as pltpu
from jax.sharding import PartitionSpec as P

NORM_EPS = 1e-5
ROPE_THETA = 1000000.0
F32 = jnp.float32
BF16 = jnp.bfloat16
TILE = 256
RING = 4


def rope_tables(positions, head_dim):
    half_dim = head_dim // 2
    inv_freq = ROPE_THETA ** (-2.0 * jnp.arange(half_dim, dtype=F32) / head_dim)
    angles = positions.astype(F32)[:, None] * inv_freq
    cosines, sines = jnp.cos(angles), jnp.sin(angles)
    return jnp.concatenate([cosines, cosines], axis=-1), jnp.concatenate([-sines, sines], axis=-1)


def rms_rows(rows_f32, gain_row):
    inv_rms = lax.rsqrt(jnp.mean(rows_f32 * rows_f32, axis=-1, keepdims=True) + NORM_EPS)
    return (rows_f32 * inv_rms * gain_row).astype(BF16)


def qkv_kernel(x_ref, gain_ref, cos_ref, sin_ref, wq, wk, wv, out_ref, h_ref, wbuf, sems):
    head_dim = cos_ref.shape[-1]
    spans = [w.shape[1] // TILE for w in (wq, wk, wv)]
    first = [0, spans[0], spans[0] + spans[1]]
    total = sum(spans)
    per_tile = TILE // head_dim

    def start(t):
        slot = lax.rem(t, RING)
        for w, lo, n in zip((wq, wk, wv), first, spans):
            @pl.when((t >= lo) & (t < lo + n))
            def _():
                col = pl.multiple_of((t - lo) * TILE, TILE)
                pltpu.make_async_copy(w.at[:, pl.ds(col, TILE)], wbuf.at[slot], sems.at[slot]).start()

    for t in range(RING - 1):
        start(jnp.int32(t))
    h_ref[...] = rms_rows(x_ref[...].astype(F32), gain_ref[...].astype(F32))

    def step(t, carry):
        slot = lax.rem(t, RING)
        start(t + RING - 1)
        pltpu.make_async_copy(wq.at[:, pl.ds(0, TILE)], wbuf.at[slot], sems.at[slot]).wait()
        acc = jnp.dot(h_ref[...], wbuf[slot], preferred_element_type=F32)
        for i in range(per_tile):
            v = acc[:, i * head_dim:(i + 1) * head_dim].astype(BF16).astype(F32)
            rot = v * cos_ref[...] + pltpu.roll(v, head_dim // 2, 1) * sin_ref[...]
            out_ref[t * per_tile + i] = jnp.where(t < first[2], rot.astype(BF16).astype(F32), v)
        return carry

    lax.fori_loop(0, total, step, 0)


def qkv_project(hidden, gain, positions, wq, wk, wv, head_dim):
    tokens, d_model = hidden.shape
    cos, sin = rope_tables(positions, head_dim)
    heads = (wq.shape[1] + wk.shape[1] + wv.shape[1]) // head_dim
    vmem = pl.BlockSpec(memory_space=pltpu.VMEM)
    hbm = pl.BlockSpec(memory_space=pl.ANY)
    return pl.pallas_call(
        qkv_kernel,
        out_shape=jax.ShapeDtypeStruct((heads, tokens, head_dim), F32),
        in_specs=[vmem] * 4 + [hbm] * 3,
        out_specs=vmem,
        scratch_shapes=[pltpu.VMEM((tokens, d_model), BF16), pltpu.VMEM((RING, d_model, TILE), BF16), pltpu.SemaphoreType.DMA((RING,))],
        compiler_params=pltpu.CompilerParams(vmem_limit_bytes=60 << 20),
    )(hidden, gain.reshape(1, -1), cos, sin, wq, wk, wv)


def attend_kernel(lens_ref, q_ref, kn_ref, vn_ref, k_ref, v_ref, ko_ref, vo_ref, o_ref):
    block, seq_len, kv_heads, head_dim = k_ref.shape
    q_heads = q_ref.shape[0]
    groups = q_heads // kv_heads
    base = pl.program_id(0) * block
    cols = seq_len * kv_heads
    lane = lax.broadcasted_iota(jnp.int32, (q_heads, cols), 1)
    row = lax.broadcasted_iota(jnp.int32, (q_heads, cols), 0)
    pos = jnp.where(lax.rem(lane, kv_heads) == row // groups, lane // kv_heads, seq_len)
    q2 = q_ref.reshape(q_heads * block, head_dim)
    kn2 = kn_ref.reshape(kv_heads * block, head_dim)
    vn2 = vn_ref.reshape(kv_heads * block, head_dim)
    o2 = o_ref.reshape(q_heads * block, head_dim)
    ko_ref[...] = k_ref[...]
    vo_ref[...] = v_ref[...]
    lens = [lens_ref[base + t] for t in range(block)]
    for t in range(block):
        ko_ref[t, lens[t]] = kn2[pl.ds(t, kv_heads, stride=block), :].astype(BF16)
        vo_ref[t, lens[t]] = vn2[pl.ds(t, kv_heads, stride=block), :].astype(BF16)
    scores = []
    for t in range(block):
        q_t = q2[pl.ds(t, q_heads, stride=block), :].astype(BF16)
        k_t = ko_ref[t].reshape(cols, head_dim)
        scores.append(lax.dot_general(q_t, k_t, (((1,), (1,)), ((), ())), preferred_element_type=F32))
    probs = []
    for t in range(block):
        s = jnp.where(pos <= lens[t], scores[t] * head_dim ** -0.5, -jnp.inf)
        e = jnp.exp(s - jnp.max(s, axis=-1, keepdims=True))
        probs.append((e / jnp.sum(e, axis=-1, keepdims=True)).astype(BF16))
    for t in range(block):
        mix = jnp.dot(probs[t], vo_ref[t].reshape(cols, head_dim), preferred_element_type=F32)
        o2[pl.ds(t, q_heads, stride=block), :] = mix.astype(BF16).astype(F32)


def attend(qkv, k_cache, v_cache, seq_lens):
    tokens, seq_len, kv_heads, head_dim = k_cache.shape
    q_heads = qkv.shape[0] - 2 * kv_heads
    block = 8
    ratio = q_heads // kv_heads
    cache = pl.BlockSpec((block, seq_len, kv_heads, head_dim), lambda i, n: (i, 0, 0, 0))
    return pl.pallas_call(
        attend_kernel,
        grid_spec=pltpu.PrefetchScalarGridSpec(
            num_scalar_prefetch=1,
            grid=(tokens // block,),
            in_specs=[
                pl.BlockSpec((q_heads, block, head_dim), lambda i, n: (0, i, 0)),
                pl.BlockSpec((kv_heads, block, head_dim), lambda i, n: (ratio, i, 0)),
                pl.BlockSpec((kv_heads, block, head_dim), lambda i, n: (ratio + 1, i, 0)),
                cache, cache],
            out_specs=[cache, cache, pl.BlockSpec((q_heads, block, head_dim), lambda i, n: (0, i, 0))],
        ),
        out_shape=[jax.ShapeDtypeStruct(k_cache.shape, BF16), jax.ShapeDtypeStruct(v_cache.shape, BF16),
                   jax.ShapeDtypeStruct((q_heads, tokens, head_dim), F32)],
        compiler_params=pltpu.CompilerParams(vmem_limit_bytes=60 << 20),
    )(seq_lens, qkv, qkv, qkv, k_cache, v_cache)


def out_kernel(x_ref, o_ref, gain_ref, ids_ref, wr_ref, wo, x1_ref, h2_ref, gates_ref, a_ref, sq_ref, wbuf, sems):
    q_heads, tokens, head_dim = o_ref.shape
    d_model = wo.shape[1]
    total = d_model // TILE

    def copy(t):
        col = pl.multiple_of(t * TILE, TILE)
        slot = lax.rem(t, RING)
        return pltpu.make_async_copy(wo.at[:, pl.ds(col, TILE)], wbuf.at[slot], sems.at[slot])

    for t in range(RING - 1):
        copy(jnp.int32(t)).start()
    for j in range(q_heads):
        a_ref[:, j * head_dim:(j + 1) * head_dim] = o_ref[j].astype(BF16)
    sq_ref[...] = jnp.zeros_like(sq_ref)

    def step(t, carry):
        @pl.when(t + RING - 1 < total)
        def _():
            copy(t + RING - 1).start()

        copy(t).wait()
        cols = pl.ds(pl.multiple_of(t * TILE, TILE), TILE)
        acc = jnp.dot(a_ref[...], wbuf[lax.rem(t, RING)], preferred_element_type=F32)
        x1 = (x_ref[:, cols].astype(F32) + acc).astype(BF16)
        x1_ref[:, cols] = x1
        x1 = x1.astype(F32)
        sq_ref[...] += x1 * x1
        return carry

    lax.fori_loop(0, total, step, 0)
    inv = lax.rsqrt(jnp.sum(sq_ref[...], axis=-1, keepdims=True) / d_model + NORM_EPS)
    h2_ref[...] = (x1_ref[...].astype(F32) * inv * gain_ref[...].astype(F32)).astype(BF16)
    logits = jnp.dot(h2_ref[...], wr_ref[...], preferred_element_type=F32)
    expert = lax.broadcasted_iota(jnp.int32, logits.shape, 1)
    p0, p1 = (jnp.sum(jnp.where(expert == ids_ref[:, k:k + 1], logits, 0.0), axis=-1, keepdims=True) for k in range(2))
    top = jnp.maximum(p0, p1)
    e0, e1 = jnp.exp(p0 - top), jnp.exp(p1 - top)
    lane = lax.broadcasted_iota(jnp.int32, gates_ref.shape, 1)
    gates_ref[...] = jnp.where(lane == 0, e0, e1) / (e0 + e1)


def out_project(hidden, mix, ffn_gain, expert_ids, w_router, w_out):
    tokens, d_model = hidden.shape
    vmem = pl.BlockSpec(memory_space=pltpu.VMEM)
    row = jax.ShapeDtypeStruct((tokens, d_model), BF16)
    return pl.pallas_call(
        out_kernel,
        out_shape=[row, row, jax.ShapeDtypeStruct((tokens, 2), F32)],
        in_specs=[vmem] * 5 + [pl.BlockSpec(memory_space=pl.ANY)],
        out_specs=[vmem] * 3,
        scratch_shapes=[pltpu.VMEM((tokens, w_out.shape[0]), BF16), pltpu.VMEM((tokens, TILE), F32),
                        pltpu.VMEM((RING, w_out.shape[0], TILE), BF16), pltpu.SemaphoreType.DMA((RING,))],
        compiler_params=pltpu.CompilerParams(vmem_limit_bytes=60 << 20),
    )(hidden, mix, ffn_gain.reshape(1, -1), expert_ids, w_router, w_out)


def choice_slots(expert_ids, expert_list, cap_slots):
    hit_mask = expert_ids[..., None] == expert_list
    hit_counts = hit_mask.reshape(hit_mask.shape[:-3] + (-1, hit_mask.shape[-1])).astype(jnp.int32)
    before = (jnp.cumsum(hit_counts, axis=-2) - hit_counts).reshape(hit_mask.shape)
    return (hit_mask[..., None] & (before[..., None] == jnp.arange(cap_slots))).astype(jnp.bfloat16)


def solution(mesh):
    n_ep = mesh.shape['ep']
    row_spec = P(('dp', 'ep'), None)
    cache_spec = P(('dp', 'ep'), None, None, None)
    expert_spec = P('ep', None, None)
    in_specs = (row_spec, cache_spec, cache_spec, P(('dp', 'ep')), row_spec, P(), P(), P(), P(), P(), P(), P(), expert_spec, expert_spec, expert_spec)
    out_specs = (row_spec, cache_spec, cache_spec)

    def device_step(hidden, k_cache, v_cache, seq_lens, expert_ids, attn_gain, w_query, w_key, w_value, w_out, ffn_gain, w_router, w_gate, w_up, w_down):
        tokens, d_model = hidden.shape
        local_experts = w_gate.shape[0]
        n_experts = local_experts * n_ep
        cap_slots = 4 * tokens // n_experts
        head_dim = k_cache.shape[-1]
        qkv = qkv_project(hidden, attn_gain, seq_lens, w_query, w_key, w_value, head_dim)
        k_cache_new, v_cache_new, mix = attend(qkv, k_cache, v_cache, seq_lens)
        resid_out, normed_ffn, gates = out_project(hidden, mix, ffn_gain, expert_ids, w_router, w_out)
        slot_sel = choice_slots(expert_ids, jnp.arange(n_experts), cap_slots)
        send_buf = jnp.einsum('tkec,td->ecd', slot_sel, normed_ffn, preferred_element_type=jnp.float32).astype(jnp.bfloat16)
        send_buf = send_buf.reshape(n_ep, local_experts, cap_slots, d_model)
        recv_buf = lax.all_to_all(send_buf, 'ep', 0, 0, tiled=True)
        gate_act = jnp.einsum('sxcd,xdf->sxcf', recv_buf, w_gate, preferred_element_type=jnp.float32)
        up_act = jnp.einsum('sxcd,xdf->sxcf', recv_buf, w_up, preferred_element_type=jnp.float32)
        inner_act = (jax.nn.silu(gate_act) * up_act).astype(jnp.bfloat16)
        expert_out = jnp.einsum('sxcf,xfd->sxcd', inner_act, w_down, preferred_element_type=jnp.float32).astype(jnp.bfloat16)
        returned = lax.all_to_all(expert_out, 'ep', 0, 0, tiled=True).reshape(n_experts, cap_slots, d_model)
        routed = jnp.einsum('tkec,ecd->tkd', slot_sel, returned, preferred_element_type=jnp.float32)
        out_f32 = resid_out.astype(jnp.float32) + jnp.sum(gates[:, :, None] * routed, axis=1)
        return out_f32.astype(jnp.bfloat16), k_cache_new, v_cache_new

    return jax.shard_map(device_step, mesh=mesh, in_specs=in_specs, out_specs=out_specs, check_vma=False)
```

time: 232 us -> 215 us (0.927)
  matrix products: 97.1 us -> 37.7 us
  Pallas kernels: 0 us -> 55.1 us
  other arithmetic: 20.7 us -> 4.46 us
  local copies, waits for them, and re-layouts: 6.01 us -> 8.57 us
    pallas_call x0 -> x3, Pallas kernels: none -> 55.1 us  [the longest x1 20.4 us: attend(): pl.pallas_call(attend_kernel, grid_spec=pltpu.PrefetchScalarGridSpec(num_...]
    dot_general x6 -> x0, matrix products: 43.1 us -> none  [the longest x1 13.3 us: attention_block(): jnp.dot(attn_mix.reshape(tokens, q_heads * head_dim), w_out, preferred_el...]
    select_n x1 -> x0, other arithmetic: 11.9 us -> none  [attention_block(): k_cache_new = jnp.where(slot_hit, key_new[:, None], k_cache)]
    sub x1 -> x0, matrix products: 9.38 us -> none  [attention_block(): jax.nn.softmax(jnp.where(visible, scores, -jnp.inf), axis=-1)]
    dot_general x1, matrix products: 16.6 us -> 11.6 us  [device_step(): jnp.einsum('sxcd,xdf->sxcf', recv_buf, w_up, preferred_element_type=jnp.f...]
    dot_general x1, matrix products: 12.6 us -> 9.44 us  [device_step(): jnp.einsum('sxcd,xdf->sxcf', recv_buf, w_gate, preferred_element_type=jnp...]
where the time goes in v1:
time: 215 us; the launch traced here: 214 us
  Pallas kernels  55.1 us (26%)
  blocking collectives  54.1 us (25%)
  waiting for transfers between devices  48.9 us (23%)
  matrix products  37.7 us (18%)
  local copies, waits for them, and re-layouts  8.57 us (4%)
  starting transfers between devices  4.68 us (2%)
  other arithmetic  4.46 us (2%)
    all_to_all x1, blocking collectives, device_step(): recv_buf = lax.all_to_all(send_buf, 'ep', 0, 0, tiled=True)  54.1 us
    all_to_all x1, waiting for transfers between devices, device_step(): lax.all_to_all(expert_out, 'ep', 0, 0, tiled=True)  48.9 us
    pallas_call x1, Pallas kernels, attend(): pl.pallas_call(attend_kernel, grid_spec=pltpu.PrefetchScalarGridSpec(num_...  20.4 us
    pallas_call x1, Pallas kernels, qkv_project(): pl.pallas_call(qkv_kernel, out_shape=jax.ShapeDtypeStruct((heads, tokens,...  19.5 us
    pallas_call x1, Pallas kernels, out_project(): pl.pallas_call(out_kernel, out_shape=[row, row, jax.ShapeDtypeStruct((tok...  15.3 us
    dot_general x1, matrix products, device_step(): jnp.einsum('sxcd,xdf->sxcf', recv_buf, w_up, preferred_element_type=jnp.f...  11.6 us
    dot_general x1, matrix products, device_step(): jnp.einsum('sxcf,xfd->sxcd', inner_act, w_down, preferred_element_type=jn...  10.3 us
    dot_general x1, matrix products, device_step(): jnp.einsum('sxcd,xdf->sxcf', recv_buf, w_gate, preferred_element_type=jnp...  9.44 us
  transfers between devices with their start and end apart: 1, of which 1 were waited for; matrix products, arithmetic and copies ran while one was open for 0% of the time, Pallas kernels for 0%

profile of v1, /device:TPU:0, one launch (start us, length us, event | category | flops | bytes accessed | tf_op | source)
XLA Modules:
  0.0 214.2 jit_solution(5921003276403669666)
XLA Ops:
  0.6 0.7 iota_compare_fusion.3
  1.3 0.8 copy.32.ids_ref
  2.1 0.1 eq.58
  2.3 0.1 eq.54
  2.4 0.7 convert_element_type.34
  3.1 1.3 reshape.46.gain_ref
  4.4 1.3 reshape.47.gain_ref
  5.7 0.6 reduce-window.6
  6.2 0.2 slice_reduce_fusion
  6.5 0.1 fusion.31
  6.6 0.1 copy.38
  6.7 0.1 copy.39
  6.7 2.2 %copy.33.wr_ref = bf16[4096,16]{1,0:T(8,128)(2,1)} copy(bf16[4096,16]{0,1:T(8,128)(2,1)} %param.26) | data formatting | bytes 262144 | tf_op args[11]
  9.0 0.1 convert_reduce_fusion
  9.1 0.3 fusion.30
  9.4 0.8 pad_maximum_fusion
  10.2 19.5 %shard_map.166.q_ref.kn_ref.vn_ref = f32[48,128,128]{2,1,0:T(8,128)} custom-call(bf16[128,4096]{1,0:T(8,128)(2,1)} %x_ref.3, bf16[1,4096]{1,0:T(2,128)(2,1)} %reshape.46.gain_ref, f32[128,128]{1,0:T(8,128)} %get-tuple-element.18.cos_ref, f32[128,128]{1,0:T(8,128)} %get-tuple-element.19.sin_ref, bf16[4096,4096]{1,0:T(8,128)(2,1)} %wq.1, ...), custom_call_target="tpu_custom_call" | custom-call | tf_op jit(solution)/shard_map/pallas_call | solution.py:70
  29.7 0.0 copy-done
  29.7 20.4 %shard_map.167 = (bf16[128,32,8,128]{3,2,1,0:T(8,128)(2,1)}, bf16[128,32,8,128]{3,2,1,0:T(8,128)(2,1)}, f32[32,128,128]{2,1,0:T(8,128)}) custom-call(s32[128]{0:T(128)} %lens_ref.1, f32[48,128,128]{2,1,0:T(8,128)} %shard_map.166.q_ref.kn_ref.vn_ref, f32[48,128,128]{2,1,0:T(8,128)} %shard_map.166.q_ref.kn_ref.vn_ref, ...), custom_call_target="tpu_custom_call" | custom-call | tf_op jit(solution)/shard_map/pallas_call | solution.py:120
  50.0 15.3 %shard_map.168 = (bf16[128,4096]{1,0:T(8,128)(2,1)}, bf16[128,4096]{1,0:T(8,128)(2,1)}, f32[128,2]{1,0:T(8,128)}) custom-call(bf16[128,4096]{1,0:T(8,128)(2,1)} %x_ref.3, f32[32,128,128]{2,1,0:T(8,128)} %get-tuple-element.9.o_ref, bf16[1,4096]{1,0:T(2,128)(2,1)} %reshape.47.gain_ref, s32[128,2]{1,0:T(8,128)} %copy-done, bf16[4096,16]{1,0:T(8,128)(2,1)} %copy.33.wr_ref, ...), custom_call_target="tpu_custom_call" | custom-call | tf_op jit(solution)/shard_map/pallas_call | solution.py:184
  65.3 2.5 %convolution_convert_fusion = bf16[16,32,4096]{2,1,0:T(8,128)(2,1)S(1)} fusion(bf16[128,16,32]{0,2,1:T(8,128)(2,1)S(1)} %convert_reduce_fusion, bf16[128,4096]{1,0:T(8,128)(2,1)} %get-tuple-element.12), kind=kOutput, calls=%fused_computation.7 | convolution fusion | flops 536870912 | bytes 5373952 | tf_op jit(solution)/shard_map/tkec,td->ecd/dot_general | solution.py:220
  67.8 54.1 %all_to_all.10 = bf16[8,2,32,4096]{3,2,1,0:T(8,128)(2,1)} all-to-all(bf16[8,2,32,4096]{3,2,1,0:T(8,128)(2,1)S(1)} %bitcast.69), channel_id=1, replica_groups=mesh['dp'=4,'ep'=8] {'ep'}, dimensions={0} | all-to-all | bytes 8388608 | tf_op jit(solution)/shard_map/all_to_all | solution.py:222
  121.8 9.4 %fusion.4 = f32[2,8,32,960]{3,2,1,0:T(8,128)S(1)} fusion(bf16[2,4096,960]{1,2,0:T(8,128)(2,1)} %param.27, bf16[8,2,32,4096]{3,2,1,0:T(8,128)(2,1)} %all_to_all.10), kind=kOutput, calls=%fused_computation.4 | convolution fusion | flops 4026531840 | bytes 21889024 | tf_op jit(solution)/shard_map/sxcd,xdf->sxcf/dot_general | solution.py:223
  131.3 11.6 %fusion.15 = bf16[8,2,32,960]{3,2,0,1:T(8,128)(2,1)S(1)} fusion(f32[2,8,32,960]{3,2,1,0:T(8,128)S(1)} %fusion.4, bf16[2,4096,960]{1,2,0:T(8,128)(2,1)} %param.28, bf16[8,2,32,4096]{3,2,1,0:T(8,128)(2,1)} %all_to_all.10), kind=kOutput, calls=%fused_computation.14 | convolution fusion | flops 4029480960 | bytes 22872064 | tf_op jit(solution)/shard_map/sxcd,xdf->sxcf/dot_general | solution.py:224
  142.9 10.3 %fusion.9 = bf16[8,2,32,4096]{3,2,0,1:T(8,128)(2,1)S(1)} fusion(bf16[8,2,32,960]{3,2,0,1:T(8,128)(2,1)S(1)} %fusion.15, bf16[2,960,4096]{2,1,0:T(8,128)(2,1)} %param.29), kind=kOutput, calls=%fused_computation.8 | convolution fusion | flops 4028628992 | bytes 20905984 | tf_op jit(solution)/shard_map/sxcf,xfd->sxcd/dot_general | solution.py:226
  153.2 2.2 %copy.42 = bf16[8,2,32,4096]{3,2,1,0:T(8,128)(2,1)} copy(bf16[8,2,32,4096]{3,2,0,1:T(8,128)(2,1)S(1)} %fusion.9) | data formatting | bytes 8388608 | tf_op jit(solution)/shard_map/convert_element_type | solution.py:226
  155.4 4.7 %all-to-all-start.1 = ((bf16[8,2,32,4096]{3,2,1,0:T(8,128)(2,1)}), bf16[8,2,32,4096]{3,2,1,0:T(8,128)(2,1)}, u32[]{:S(2)}, u32[]{:S(2)}) async-start(bf16[8,2,32,4096]{3,2,1,0:T(8,128)(2,1)} %copy.42), calls=%async_computation.1 | async-start | bytes 8388608 | tf_op jit(solution)/shard_map/all_to_all | solution.py:227
  160.1 0.0 copy-start.1
  160.1 0.1 copy.34
  160.2 48.9 %all-to-all-done.1 = bf16[8,2,32,4096]{3,2,1,0:T(8,128)(2,1)} async-done(((bf16[8,2,32,4096]{3,2,1,0:T(8,128)(2,1)}), bf16[8,2,32,4096]{3,2,1,0:T(8,128)(2,1)}, u32[]{:S(2)}, u32[]{:S(2)}) %all-to-all-start.1) | async-done | bytes 4194336 | tf_op jit(solution)/shard_map/all_to_all | solution.py:227
  209.1 3.9 %fusion.19 = f32[128,4096]{1,0:T(8,128)S(1)} fusion(bf16[16,32,4096,1]{2,1,0,3:T(8,128)(2,1)} %bitcast.14, f32[128,2]{0,1:T(2,128)S(1)} %copy.34, s32[128,2,16]{0,2,1:T(8,128)S(1)} %copy.39, pred[128,2,16]{0,2,1:T(8,128)(4,1)S(1)} %iota_compare_fusion.3), kind=kOutput, calls=%fused_computation.21 | convolution fusion | flops 1075576832 | bytes 6312960 | tf_op jit(solution)/shard_map/tkec,ecd->tkd/dot_general | solution.py:228
  213.0 1.2 add_convert_fusion
  (8 shorter events, 0.1 us)
Async XLA Ops:
  2.1 27.6 %copy-start = (s32[128,2]{1,0:T(8,128)}, s32[128,2]{1,0:T(8,128)S(1)}, u32[]{:S(2)}) copy-start(s32[128,2]{1,0:T(8,128)S(1)} %copy.32.ids_ref) | copy-start | bytes 3076
  155.4 4.7 %copy-start.2 = (f32[128,2]{1,0:T(8,128)S(1)}, f32[128,2]{1,0:T(8,128)}, u32[]{:S(2)}) copy-start(f32[128,2]{1,0:T(8,128)} %get-tuple-element.11) | copy-start | bytes 3076
  155.4 53.7 %all-to-all-start.1 = ((bf16[8,2,32,4096]{3,2,1,0:T(8,128)(2,1)}), bf16[8,2,32,4096]{3,2,1,0:T(8,128)(2,1)}, u32[]{:S(2)}, u32[]{:S(2)}) async-start(bf16[8,2,32,4096]{3,2,1,0:T(8,128)(2,1)} %copy.42), calls=%async_computation.1 | async-start | bytes 8388608 | tf_op jit(solution)/shard_map/all_to_all | solution.py:227
  160.1 52.9 %copy-start.1 = (bf16[128,4096]{1,0:T(8,128)(2,1)S(1)}, bf16[128,4096]{1,0:T(8,128)(2,1)}, u32[]{:S(2)}) copy-start(bf16[128,4096]{1,0:T(8,128)(2,1)} %get-tuple-element.10) | copy-start | bytes 3145732

commit v2 on v1

--- a/solution.py
+++ b/solution.py
@@ -13,6 +13,7 @@
 BF16 = jnp.bfloat16
 TILE = 256
 RING = 4
+CHUNKS = 4
 
 
 def rope_tables(positions, head_dim):
@@ -167,8 +168,12 @@
 
     lax.fori_loop(0, total, step, 0)
     inv = lax.rsqrt(jnp.sum(sq_ref[...], axis=-1, keepdims=True) / d_model + NORM_EPS)
-    h2_ref[...] = (x1_ref[...].astype(F32) * inv * gain_ref[...].astype(F32)).astype(BF16)
-    logits = jnp.dot(h2_ref[...], wr_ref[...], preferred_element_type=F32)
+    chunks, _, width = h2_ref.shape
+    logits = jnp.zeros((tokens, wr_ref.shape[0]), F32)
+    for q in range(chunks):
+        cols = slice(q * width, (q + 1) * width)
+        h2_ref[q] = (x1_ref[:, cols].astype(F32) * inv * gain_ref[:, cols].astype(F32)).astype(BF16)
+        logits += lax.dot_general(h2_ref[q], wr_ref[:, cols], (((1,), (1,)), ((), ())), preferred_element_type=F32)
     expert = lax.broadcasted_iota(jnp.int32, logits.shape, 1)
     p0, p1 = (jnp.sum(jnp.where(expert == ids_ref[:, k:k + 1], logits, 0.0), axis=-1, keepdims=True) for k in range(2))
     top = jnp.maximum(p0, p1)
@@ -183,20 +188,183 @@
     row = jax.ShapeDtypeStruct((tokens, d_model), BF16)
     return pl.pallas_call(
         out_kernel,
-        out_shape=[row, row, jax.ShapeDtypeStruct((tokens, 2), F32)],
+        out_shape=[row, jax.ShapeDtypeStruct((CHUNKS, tokens, d_model // CHUNKS), BF16), jax.ShapeDtypeStruct((tokens, 2), F32)],
         in_specs=[vmem] * 5 + [pl.BlockSpec(memory_space=pl.ANY)],
         out_specs=[vmem] * 3,
         scratch_shapes=[pltpu.VMEM((tokens, w_out.shape[0]), BF16), pltpu.VMEM((tokens, TILE), F32),
                         pltpu.VMEM((RING, w_out.shape[0], TILE), BF16), pltpu.SemaphoreType.DMA((RING,))],
         compiler_params=pltpu.CompilerParams(vmem_limit_bytes=60 << 20),
-    )(hidden, mix, ffn_gain.reshape(1, -1), expert_ids, w_router, w_out)
-
-
-def choice_slots(expert_ids, expert_list, cap_slots):
-    hit_mask = expert_ids[..., None] == expert_list
-    hit_counts = hit_mask.reshape(hit_mask.shape[:-3] + (-1, hit_mask.shape[-1])).astype(jnp.int32)
-    before = (jnp.cumsum(hit_counts, axis=-2) - hit_counts).reshape(hit_mask.shape)
-    return (hit_mask[..., None] & (before[..., None] == jnp.arange(cap_slots))).astype(jnp.bfloat16)
+    )(hidden, mix, ffn_gain.reshape(1, -1), expert_ids, w_router.T, w_out)
+
+
+def moe_kernel(n_ep, h_ref, x1_ref, gates_ref, codes_ref, code_cols_ref, wg, wu, wd, out_ref,
+               buf, x_ref, y_in, act_ref, sum_ref, codes_in, wbuf, wsem, csend, crecv, gsend, grecv, ysend, yrecv):
+    me = lax.axis_index('ep')
+    bits = [lax.rem(me, 2), lax.rem(me // 2, 2), me // 4]
+    chunks, tokens, width = h_ref.shape
+    d_model = chunks * width
+    local_experts, rows_all, _ = x_ref.shape
+    cap = rows_all // n_ep
+    d_ff = wd.shape[1]
+
+    def peer(r):
+        return me + sum(((r >> b) & 1) * (1 << b) * (1 - 2 * bits[b]) for b in range(3))
+
+    def remote(src, dst, send, recv, r):
+        return pltpu.make_async_remote_copy(src_ref=src, dst_ref=dst, send_sem=send, recv_sem=recv, device_id={'ep': peer(r)},
+                                            device_id_type=pl.DeviceIdType.MESH)
+
+    def block(r, q):
+        return h_ref.at[q] if r == 0 else buf.at[r - 1, q]
+
+    def push(slot, q):
+        if slot in (2, 4):
+            src, to = 0, slot
+        elif slot == 6:
+            src, to = (2, 4) if q < chunks // 2 else (4, 2)
+        else:
+            src, to = slot - 1, 1
+        return remote(block(src, q), buf.at[slot - 1, q], gsend.at[slot, q], grecv.at[slot, q], to)
+
+    def weight(i):
+        e, m = i // 3, i % 3
+        slot = i if i < 5 else 0
+        return pltpu.make_async_copy((wg, wu, wd)[m].at[e], wbuf.at[slot], wsem.at[i])
+
+    def code_copy(r):
+        return remote(codes_ref, codes_in.at[r], csend.at[r], crecv.at[r], r)
+
+    for i in range(5):
+        weight(i).start()
+    barrier = pltpu.get_barrier_semaphore()
+    for r in range(1, n_ep):
+        pl.semaphore_signal(barrier, inc=1, device_id={'ep': peer(r)}, device_id_type=pl.DeviceIdType.MESH)
+    pl.semaphore_wait(barrier, n_ep - 1)
+
+    for r in range(1, n_ep):
+        code_copy(r).start()
+    for q in range(chunks):
+        push(2, q).start()
+        push(4, q).start()
+    for q in range(chunks):
+        push(1, q).start()
+
+    slot_iota = lax.broadcasted_iota(jnp.int32, (local_experts * cap, tokens), 0)
+    picks = {}
+
+    def select(r, q):
+        if r not in picks:
+            if r:
+                code_copy(r).wait_recv()
+            codes = codes_ref[...] if r == 0 else codes_in[r]
+            want = (slot_iota + me * (local_experts * cap)).astype(F32)
+            hit = (jnp.broadcast_to(codes[0:1], want.shape) == want) | (jnp.broadcast_to(codes[1:2], want.shape) == want)
+            picks[r] = jnp.where(hit, 1.0, 0.0).astype(BF16)
+        got = jnp.dot(picks[r], block(r, q)[...], preferred_element_type=F32).astype(BF16)
+        for e in range(local_experts):
+            x_ref[e, r * cap:(r + 1) * cap, q * width:(q + 1) * width] = got[e * cap:(e + 1) * cap]
+
+    for q in range(chunks):
+        select(0, q)
+    for q in range(chunks):
+        for slot in (2, 4):
+            push(slot, q).wait_recv()
+            if (slot == 2) == (q < chunks // 2):
+                push(6, q).start()
+            push(slot + 1, q).start()
+        for slot in (1, 2, 4):
+            if slot == 1:
+                push(slot, q).wait_recv()
+            select(slot, q)
+    for q in range(chunks):
+        for slot in (3, 5):
+            push(slot, q).wait_recv()
+            select(slot, q)
+    for q in (0, chunks // 2, 1, chunks // 2 + 1):
+        push(6, q).wait_recv()
+        push(7, q).start()
+        select(6, q)
+    for q in (0, chunks // 2, 1, chunks // 2 + 1):
+        push(7, q).wait_recv()
+        select(7, q)
+
+    def y_copy(e, r):
+        rows = pl.ds(r * cap, cap)
+        return remote(x_ref.at[e, rows], y_in.at[e, rows], ysend.at[e, r], yrecv.at[e, r], r)
+
+    order = (6, 7, 2, 4, 3, 5, 1)
+    for e in range(local_experts):
+        base = 3 * e
+        slots = [i if i < 5 else 0 for i in range(base, base + 3)]
+        weight(base).wait()
+        weight(base + 1).wait()
+        for lo in range(0, d_ff, 256):
+            hi = min(lo + 256, d_ff)
+            gate, up = (lax.dot_general(x_ref[e], wbuf[s, lo:hi], (((1,), (1,)), ((), ())), preferred_element_type=F32) for s in slots[:2])
+            act_ref[:, lo:hi] = (gate * jax.nn.sigmoid(gate) * up).astype(BF16)
+        if e == 0:
+            weight(5).start()
+        weight(base + 2).wait()
+        for lo in range(0, d_model, 512):
+            x_ref[e, :, lo:lo + 512] = jnp.dot(act_ref[...], wbuf[slots[2], :, lo:lo + 512], preferred_element_type=F32).astype(BF16)
+        for r in order:
+            y_copy(e, r).start()
+        y_in[e, 0:cap] = x_ref[e, 0:cap]
+
+    lane = lax.broadcasted_iota(jnp.int32, (tokens, rows_all), 1)
+    rel, rank = lane // cap, lax.rem(lane, cap)
+    owner = me + sum(lax.rem(rel // (1 << b), 2) * (1 << b) * (1 - 2 * bits[b]) for b in range(3))
+    for e in range(local_experts):
+        for r in range(1, n_ep):
+            y_copy(e, r).wait_recv()
+        want = ((owner * local_experts + e) * cap + rank).astype(F32)
+        sel = [jnp.where(code_cols_ref[:, k:k + 1] == want, 1.0, 0.0).astype(BF16) for k in range(2)]
+        for lo in range(0, d_model, 512):
+            y = y_in[e, :, lo:lo + 512]
+            part = sum(gates_ref[:, k:k + 1] * jnp.dot(sel[k], y, preferred_element_type=F32) for k in range(2))
+            if e < local_experts - 1:
+                sum_ref[:, lo:lo + 512] = part
+            else:
+                out_ref[:, lo:lo + 512] = (x1_ref[:, lo:lo + 512].astype(F32) + (sum_ref[:, lo:lo + 512] + part)).astype(BF16)
+
+    for r in range(1, n_ep):
+        code_copy(r).wait_send()
+        for q in range(chunks):
+            push(r, q).wait_send()
+        for e in range(local_experts):
+            y_copy(e, r).wait_send()
+
+
+def moe(h2, x1, gates, expert_ids, w_gate, w_up, w_down, n_ep, cap):
+    chunks, tokens, width = h2.shape
+    d_model = chunks * width
+    local_experts, d_ff, _ = w_down.shape
+    hits = (expert_ids[:, :, None] == jnp.arange(n_ep * local_experts)).astype(F32)
+    counts = jnp.sum(hits, axis=1)
+    before = jnp.dot(jnp.tril(jnp.ones((tokens, tokens), F32), -1), counts, precision=lax.Precision.HIGHEST)
+    code_cols = expert_ids.astype(F32) * cap + jnp.sum(hits * before[:, None, :], axis=-1)
+    codes = jnp.zeros((8, tokens), F32).at[:2].set(code_cols.T)
+    vmem = pl.BlockSpec(memory_space=pltpu.VMEM)
+    hbm = pl.BlockSpec(memory_space=pl.ANY)
+    rows = n_ep * cap
+    dma = pltpu.SemaphoreType.DMA
+    return pl.pallas_call(
+        functools.partial(moe_kernel, n_ep),
+        out_shape=jax.ShapeDtypeStruct((tokens, d_model), BF16),
+        in_specs=[vmem] * 5 + [hbm] * 3,
+        out_specs=vmem,
+        scratch_shapes=[
+            pltpu.VMEM((n_ep - 1, chunks, tokens, width), BF16),
+            pltpu.VMEM((local_experts, rows, d_model), BF16),
+            pltpu.VMEM((local_experts, rows, d_model), BF16),
+            pltpu.VMEM((rows, d_ff), BF16),
+            pltpu.VMEM((tokens, d_model), F32),
+            pltpu.VMEM((n_ep, 8, tokens), F32),
+            pltpu.VMEM((5, d_ff, d_model), BF16),
+            dma((6,)), dma((n_ep,)), dma((n_ep,)), dma((n_ep, chunks)), dma((n_ep, chunks)), dma((local_experts, n_ep)), dma((local_experts, n_ep)),
+        ],
+        compiler_params=pltpu.CompilerParams(vmem_limit_bytes=67043328, collective_id=0, has_side_effects=True),
+    )(h2, x1, gates, codes, code_cols, jnp.swapaxes(w_gate, 1, 2), jnp.swapaxes(w_up, 1, 2), w_down)
 
 
 def solution(mesh):
@@ -216,17 +384,7 @@
         qkv = qkv_project(hidden, attn_gain, seq_lens, w_query, w_key, w_value, head_dim)
         k_cache_new, v_cache_new, mix = attend(qkv, k_cache, v_cache, seq_lens)
         resid_out, normed_ffn, gates = out_project(hidden, mix, ffn_gain, expert_ids, w_router, w_out)
-        slot_sel = choice_slots(expert_ids, jnp.arange(n_experts), cap_slots)
-        send_buf = jnp.einsum('tkec,td->ecd', slot_sel, normed_ffn, preferred_element_type=jnp.float32).astype(jnp.bfloat16)
-        send_buf = send_buf.reshape(n_ep, local_experts, cap_slots, d_model)
-        recv_buf = lax.all_to_all(send_buf, 'ep', 0, 0, tiled=True)
-        gate_act = jnp.einsum('sxcd,xdf->sxcf', recv_buf, w_gate, preferred_element_type=jnp.float32)
-        up_act = jnp.einsum('sxcd,xdf->sxcf', recv_buf, w_up, preferred_element_type=jnp.float32)
-        inner_act = (jax.nn.silu(gate_act) * up_act).astype(jnp.bfloat16)
-        expert_out = jnp.einsum('sxcf,xfd->sxcd', inner_act, w_down, preferred_element_type=jnp.float32).astype(jnp.bfloat16)
-        returned = lax.all_to_all(expert_out, 'ep', 0, 0, tiled=True).reshape(n_experts, cap_slots, d_model)
-        routed = jnp.einsum('tkec,ecd->tkd', slot_sel, returned, preferred_element_type=jnp.float32)
-        out_f32 = resid_out.astype(jnp.float32) + jnp.sum(gates[:, :, None] * routed, axis=1)
-        return out_f32.astype(jnp.bfloat16), k_cache_new, v_cache_new
+        out = moe(normed_ffn, resid_out, gates, expert_ids, w_gate, w_up, w_down, n_ep, cap_slots)
+        return out, k_cache_new, v_cache_new
 
     return jax.shard_map(device_step, mesh=mesh, in_specs=in_specs, out_specs=out_specs, check_vma=False)

time: 215 us -> 165 us (0.77)
  Pallas kernels: 55.1 us -> 155 us
  blocking collectives: 54.1 us -> 0 us
  waiting for transfers between devices: 48.9 us -> 0 us
  matrix products: 37.7 us -> 0.25 us
  starting transfers between devices: 4.68 us -> 0 us
  other arithmetic: 4.46 us -> 1.82 us
  local copies, waits for them, and re-layouts: 8.57 us -> 6.31 us
    pallas_call x1 -> x2, Pallas kernels: 15.3 us -> 115 us  [the longest x1 100 us: moe(): pl.pallas_call(functools.partial(moe_kernel, n_ep), out_shape=jax.ShapeDt...]
    all_to_all x1 -> x0, blocking collectives: 54.1 us -> none  [device_step(): recv_buf = lax.all_to_all(send_buf, 'ep', 0, 0, tiled=True)]
    all_to_all x1 -> x0, waiting for transfers between devices: 48.9 us -> none  [device_step(): lax.all_to_all(expert_out, 'ep', 0, 0, tiled=True)]
    dot_general x5 -> x1, matrix products: 37.7 us -> 0.25 us  [moe(): jnp.dot(jnp.tril(jnp.ones((tokens, tokens), F32), -1), counts, precision=...]
    all_to_all x1 -> x0, starting transfers between devices: 4.68 us -> none  [device_step(): lax.all_to_all(expert_out, 'ep', 0, 0, tiled=True)]
    convert_element_type x1 -> x0, local copies, waits for them, and re-layouts: 2.24 us -> none  [device_step(): jnp.einsum('sxcf,xfd->sxcd', inner_act, w_down, preferred_element_type=jn...]
  transfers between devices with their start and end apart: 1 -> 0, of which waited for: 1 -> 0; matrix products, arithmetic and copies ran while one was open for 0% -> 0% of each run, Pallas kernels for 0% -> 0%
where the time goes in v2:
time: 165 us; the launch traced here: 164 us
  Pallas kernels  155 us (94%)
  local copies, waits for them, and re-layouts  6.31 us (4%)
  other arithmetic  1.82 us (1%)
    pallas_call x1, Pallas kernels, moe(): pl.pallas_call(functools.partial(moe_kernel, n_ep), out_shape=jax.ShapeDt...  100 us
    pallas_call x1, Pallas kernels, attend(): pl.pallas_call(attend_kernel, grid_spec=pltpu.PrefetchScalarGridSpec(num_...  20.5 us
    pallas_call x1, Pallas kernels, qkv_project(): pl.pallas_call(qkv_kernel, out_shape=jax.ShapeDtypeStruct((heads, tokens,...  19.5 us
    pallas_call x1, Pallas kernels, out_project(): pl.pallas_call(out_kernel, out_shape=[row, jax.ShapeDtypeStruct((CHUNKS,...  15 us

profile of v2, /device:TPU:0, one launch (start us, length us, event | category | flops | bytes accessed | tf_op | source)
XLA Modules:
  0.0 164.1 jit_solution(8804812922067890520)
XLA Ops:
  0.6 0.7 convert_element_type.9
  1.3 0.3 fusion.5
  1.6 0.8 pad_maximum_fusion
  2.4 1.3 reshape.46.gain_ref
  3.7 19.5 %shard_map.166.q_ref.kn_ref.vn_ref = f32[48,128,128]{2,1,0:T(8,128)} custom-call(bf16[128,4096]{1,0:T(8,128)(2,1)} %x_ref.3, bf16[1,4096]{1,0:T(2,128)(2,1)} %reshape.46.gain_ref, f32[128,128]{1,0:T(8,128)} %get-tuple-element.30.cos_ref, f32[128,128]{1,0:T(8,128)} %get-tuple-element.31.sin_ref, bf16[4096,4096]{1,0:T(8,128)(2,1)} %wq.1, ...), custom_call_target="tpu_custom_call" | custom-call | tf_op jit(solution)/shard_map/pallas_call | solution.py:71
  23.2 0.0 copy-start
  23.2 0.0 copy-start.1
  23.2 20.5 %shard_map.167 = (bf16[128,32,8,128]{3,2,1,0:T(8,128)(2,1)}, bf16[128,32,8,128]{3,2,1,0:T(8,128)(2,1)}, f32[32,128,128]{2,1,0:T(8,128)}) custom-call(s32[128]{0:T(128)} %lens_ref.1, f32[48,128,128]{2,1,0:T(8,128)} %shard_map.166.q_ref.kn_ref.vn_ref, f32[48,128,128]{2,1,0:T(8,128)} %shard_map.166.q_ref.kn_ref.vn_ref, ...), custom_call_target="tpu_custom_call" | custom-call | tf_op jit(solution)/shard_map/pallas_call | solution.py:121
  43.7 0.0 copy-done
  43.7 0.7 copy.29.ids_ref
  44.5 0.0 copy-done.1
  44.5 0.6 reshape.47.gain_ref
  45.1 15.0 %shard_map.168 = (bf16[128,4096]{1,0:T(8,128)(2,1)}, bf16[4,128,1024]{2,1,0:T(8,128)(2,1)}, f32[128,2]{1,0:T(8,128)}) custom-call(bf16[128,4096]{1,0:T(8,128)(2,1)} %x_ref.3, f32[32,128,128]{2,1,0:T(8,128)} %get-tuple-element.21.o_ref, bf16[1,4096]{1,0:T(2,128)(2,1)} %reshape.47.gain_ref, s32[128,2]{1,0:T(8,128)} %copy.29.ids_ref, bf16[16,4096]{1,0:T(8,128)(2,1)} %bitcast.7, ...), custom_call_target="tpu_custom_call" | custom-call | tf_op jit(solution)/shard_map/pallas_call | solution.py:189
  60.1 0.2 fusion
  60.4 0.1 select_reduce_fusion
  60.5 0.8 copy.30.code_cols_ref
  61.2 0.6 scatter.4.codes_ref
  61.8 100.0 %shard_map.169 = bf16[128,4096]{1,0:T(8,128)(2,1)} custom-call(bf16[4,128,1024]{2,1,0:T(8,128)(2,1)} %get-tuple-element.22.h_ref, bf16[128,4096]{1,0:T(8,128)(2,1)} %get-tuple-element.23.x1_ref, f32[128,2]{1,0:T(8,128)} %get-tuple-element.24.gates_ref, f32[8,128]{1,0:T(8,128)} %scatter.4.codes_ref, f32[128,2]{1,0:T(8,128)} %copy.30.code_cols_ref, ...), custom_call_target="tpu_custom_call" | custom-call | tf_op jit(solution)/shard_map/pallas_call | solution.py:351
  161.8 2.3 %copy.32 = bf16[128,4096]{1,0:T(8,128)(2,1)} copy(bf16[128,4096]{1,0:T(8,128)(2,1)} %shard_map.169) | data formatting | bytes 2097152
  (4 shorter events, 0.0 us)
Async XLA Ops:
  23.2 20.6 %copy-start = (s32[128,2]{0,1:T(2,128)S(1)}, s32[128,2]{0,1:T(2,128)}, u32[]{:S(2)}) copy-start(s32[128,2]{0,1:T(2,128)} %param.21) | copy-start | bytes 3076
  23.2 21.3 %copy-start.1 = (bf16[4096]{0:T(1024)(128)(2,1)S(1)}, bf16[4096]{0:T(1024)(128)(2,1)}, u32[]{:S(2)}) copy-start(bf16[4096]{0:T(1024)(128)(2,1)} %param.27) | copy-start | bytes 24580

commit v3 on v2

v3 whole, which is shorter than its diff:
```python
import functools

import jax
import jax.numpy as jnp
from jax import lax
from jax.experimental import pallas as pl
from jax.experimental.pallas import tpu as pltpu
from jax.sharding import PartitionSpec as P

NORM_EPS = 1e-5
ROPE_THETA = 1000000.0
F32 = jnp.float32
BF16 = jnp.bfloat16
TILE = 256
RING = 12
CHUNKS = 4


def rms_rows(rows_f32, gain_row):
    inv_rms = lax.rsqrt(jnp.mean(rows_f32 * rows_f32, axis=-1, keepdims=True) + NORM_EPS)
    return (rows_f32 * inv_rms * gain_row).astype(BF16)


def attend_kernel(lens_ref, x_ref, gain_ref, freq_ref, wq, wk, wv, k_hbm, v_hbm, ko_hbm, vo_hbm, mix_ref,
                  h_ref, cos_ref, sin_ref, qkv_ref, o_ref, kc, vc, wbuf, wsems, in_sems, out_sems):
    tokens, seq_len, kv_heads, head_dim = kc.shape
    q_heads = wq.shape[1] // head_dim
    groups = q_heads // kv_heads
    spans = [w.shape[1] // TILE for w in (wq, wk, wv)]
    first = [0, spans[0], spans[0] + spans[1]]
    total = sum(spans)
    per_tile = TILE // head_dim
    n_parts = in_sems.shape[1]
    part = tokens // n_parts
    block = o_ref.shape[1]

    def cache_in(i, w):
        rows = pl.ds(i * part, part)
        return pltpu.make_async_copy((k_hbm, v_hbm)[w].at[rows], (kc, vc)[w].at[rows], in_sems.at[w, i])

    def cache_out(i, w):
        rows = pl.ds(i * part, part)
        return pltpu.make_async_copy((kc, vc)[w].at[rows], (ko_hbm, vo_hbm)[w].at[rows], out_sems.at[w, i])

    def start(t):
        slot = lax.rem(t, RING)
        for w, lo, n in zip((wq, wk, wv), first, spans):
            @pl.when((t >= lo) & (t < lo + n))
            def _():
                col = pl.multiple_of((t - lo) * TILE, TILE)
                pltpu.make_async_copy(w.at[:, pl.ds(col, TILE)], wbuf.at[slot], wsems.at[slot]).start()

        @pl.when((t >= total) & (t < total + n_parts))
        def _():
            for w in range(2):
                cache_in(t - total, w).start()

    for t in range(RING - 1):
        start(jnp.int32(t))
    h_ref[...] = rms_rows(x_ref[...].astype(F32), gain_ref[...].astype(F32).reshape(1, -1))

    def fill(t, carry):
        cos_ref[pl.ds(t, 1), :] = jnp.full((1, head_dim), lens_ref[t].astype(F32))
        return carry

    lax.fori_loop(0, tokens, fill, 0)
    angles = cos_ref[...] * freq_ref[...]
    lane = lax.broadcasted_iota(jnp.int32, angles.shape, 1)
    sines = jnp.sin(angles)
    cos_ref[...] = jnp.cos(angles)
    sin_ref[...] = jnp.where(lane < head_dim // 2, -sines, sines)

    def project(t, carry):
        slot = lax.rem(t, RING)
        start(t + RING - 1)
        pltpu.make_async_copy(wq.at[:, pl.ds(0, TILE)], wbuf.at[slot], wsems.at[slot]).wait()
        acc = jnp.dot(h_ref[...], wbuf[slot], preferred_element_type=F32)
        for i in range(per_tile):
            v = acc[:, i * head_dim:(i + 1) * head_dim].astype(BF16).astype(F32)
            rot = v * cos_ref[...] + pltpu.roll(v, head_dim // 2, 1) * sin_ref[...]
            qkv_ref[t * per_tile + i] = jnp.where(t < first[2], rot.astype(BF16).astype(F32), v)
        return carry

    lax.fori_loop(0, total, project, 0)

    cols = seq_len * kv_heads
    lane = lax.broadcasted_iota(jnp.int32, (q_heads, cols), 1)
    row = lax.broadcasted_iota(jnp.int32, (q_heads, cols), 0)
    pos = jnp.where(lax.rem(lane, kv_heads) == row // groups, lane // kv_heads, seq_len)
    flat = qkv_ref.reshape(qkv_ref.shape[0] * tokens, head_dim)
    o2 = o_ref.reshape(q_heads * block, head_dim)

    def heads_of(t, lo, n):
        return flat[pl.ds(lo * tokens + t, n, stride=tokens), :].astype(BF16)

    def attend_part(i, carry):
        for w in range(2):
            cache_in(i, w).wait()
        for b in range(part // block):
            base = i * part + b * block
            lens = [lens_ref[base + t] for t in range(block)]
            for t in range(block):
                kc[base + t, lens[t]] = heads_of(base + t, q_heads, kv_heads)
                vc[base + t, lens[t]] = heads_of(base + t, q_heads + kv_heads, kv_heads)
            scores = [lax.dot_general(heads_of(base + t, 0, q_heads), kc[base + t].reshape(cols, head_dim),
                                      (((1,), (1,)), ((), ())), preferred_element_type=F32) for t in range(block)]
            probs = []
            for t in range(block):
                s = jnp.where(pos <= lens[t], scores[t] * head_dim ** -0.5, -jnp.inf)
                e = jnp.exp(s - jnp.max(s, axis=-1, keepdims=True))
                probs.append((e / jnp.sum(e, axis=-1, keepdims=True)).astype(BF16))
            for t in range(block):
                o2[pl.ds(t, q_heads, stride=block), :] = jnp.dot(probs[t], vc[base + t].reshape(cols, head_dim), preferred_element_type=F32)
            rows = pl.ds(pl.multiple_of(base, block), block)
            for j in range(q_heads):
                mix_ref[rows, j * head_dim:(j + 1) * head_dim] = o_ref[j].astype(BF16)
        for w in range(2):
            cache_out(i, w).start()
        return carry

    for t in range(total + RING - 1, total + n_parts):
        start(jnp.int32(t))
    lax.fori_loop(0, n_parts, attend_part, 0)
    for i in range(n_parts):
        for w in range(2):
            cache_out(i, w).wait()


def attend(hidden, gain, positions, wq, wk, wv, k_cache, v_cache):
    tokens, d_model = hidden.shape
    seq_len, kv_heads, head_dim = k_cache.shape[1:]
    q_dim = wq.shape[1]
    q_heads = q_dim // head_dim
    half_dim = head_dim // 2
    inv_freq = ROPE_THETA ** (-2.0 * jnp.arange(half_dim, dtype=F32) / head_dim)
    freq = jnp.concatenate([inv_freq, inv_freq]).reshape(1, head_dim)
    parts, block = 8, 8
    vmem = pl.BlockSpec(memory_space=pltpu.VMEM)
    hbm = pl.BlockSpec(memory_space=pl.ANY)
    dma = pltpu.SemaphoreType.DMA
    return pl.pallas_call(
        attend_kernel,
        out_shape=[jax.ShapeDtypeStruct(k_cache.shape, BF16), jax.ShapeDtypeStruct(v_cache.shape, BF16),
                   jax.ShapeDtypeStruct((tokens, q_dim), BF16)],
        in_specs=[pl.BlockSpec(memory_space=pltpu.SMEM), vmem, vmem, vmem] + [hbm] * 5,
        out_specs=[hbm, hbm, vmem],
        scratch_shapes=[
            pltpu.VMEM((tokens, d_model), BF16), pltpu.VMEM((tokens, head_dim), F32), pltpu.VMEM((tokens, head_dim), F32),
            pltpu.VMEM((q_heads + 2 * kv_heads, tokens, head_dim), F32), pltpu.VMEM((q_heads, block, head_dim), F32),
            pltpu.VMEM(k_cache.shape, BF16), pltpu.VMEM(v_cache.shape, BF16),
            pltpu.VMEM((RING, d_model, TILE), BF16),
            dma((RING,)), dma((2, parts)), dma((2, parts)),
        ],
        compiler_params=pltpu.CompilerParams(vmem_limit_bytes=67043328),
    )(positions, hidden, gain, freq, wq, wk, wv, k_cache, v_cache)


def moe_kernel(n_ep, n_experts, cap, x_in, mix_ref, gain_ref, wr_ref, ids_ref, wo, wg, wu, wd, out_ref,
               h_ref, buf, x_ref, y_in, act_ref, sum_ref, gates_ref, cols_ref, meta_ref, meta_in, wbuf,
               osem, wsem, csend, crecv, gsend, grecv, ysend, yrecv):
    me = lax.axis_index('ep')
    bits = [lax.rem(me, 2), lax.rem(me // 2, 2), me // 4]
    chunks, tokens, width = h_ref.shape
    d_model = chunks * width
    local_experts, rows_all, _ = x_ref.shape
    d_ff = wd.shape[1]
    q_dim = wo.shape[0]

    def peer(r):
        return me + sum(((r >> b) & 1) * (1 << b) * (1 - 2 * bits[b]) for b in range(3))

    def remote(src, dst, send, recv, r):
        return pltpu.make_async_remote_copy(src_ref=src, dst_ref=dst, send_sem=send, recv_sem=recv, device_id={'ep': peer(r)},
                                            device_id_type=pl.DeviceIdType.MESH)

    def block(r, q):
        return h_ref.at[q] if r == 0 else buf.at[r - 1, q]

    def push(slot, q):
        if slot in (2, 4):
            src, to = 0, slot
        elif slot == 6:
            src, to = (2, 4) if q < chunks // 2 else (4, 2)
        else:
            src, to = slot - 1, 1
        return remote(block(src, q), buf.at[slot - 1, q], gsend.at[slot, q], grecv.at[slot, q], to)

    groups = 8
    piece = q_dim // groups

    def piece_at(c, g):
        return wbuf.at[2 * (c % 2) + g // 4, 0:piece, (g % 4) * width:(g % 4 + 1) * width]

    def piece_copy(c, g):
        return pltpu.make_async_copy(wo.at[g * piece:(g + 1) * piece, c * width:(c + 1) * width], piece_at(c, g), osem.at[(c % 2) * groups + g])

    loads = ((0, 0, 4), (1, 0, 0), (2, 0, 1), (0, 1, 2), (1, 1, 3), (2, 1, 4), (0, 0, 2))

    def weight(i):
        m, e, slot = loads[i]
        return pltpu.make_async_copy((wg, wu, wd)[m].at[e], wbuf.at[slot], wsem.at[i])

    def meta_copy(r):
        return remote(meta_ref, meta_in.at[r], csend.at[r], crecv.at[r], r)

    for c in range(2):
        for g in range(groups):
            piece_copy(c, g).start()
    barrier = pltpu.get_barrier_semaphore()
    for r in range(1, n_ep):
        pl.semaphore_signal(barrier, inc=1, device_id={'ep': peer(r)}, device_id_type=pl.DeviceIdType.MESH)

    expert = lax.broadcasted_iota(jnp.int32, (n_experts, tokens), 0)
    hits = [jnp.where(jnp.broadcast_to(ids_ref[k:k + 1, :], expert.shape) == expert, 1.0, 0.0) for k in range(2)]
    earlier = lax.broadcasted_iota(jnp.int32, (tokens, tokens), 0) < lax.broadcasted_iota(jnp.int32, (tokens, tokens), 1)
    before = jnp.dot((hits[0] + hits[1]).astype(BF16), jnp.where(earlier, 1.0, 0.0).astype(BF16), preferred_element_type=F32)
    code = [ids_ref[k:k + 1, :].astype(F32) * cap + jnp.sum(hits[k] * before, axis=0, keepdims=True) for k in range(2)]
    meta_ref[...] = jnp.concatenate([jnp.broadcast_to(c, (1, tokens)) for c in code] + [jnp.zeros((6, tokens), F32)], axis=0)
    cols_ref[...] = jnp.concatenate([meta_ref[...]] * (tokens // 8), axis=0).T

    pl.semaphore_wait(barrier, n_ep - 1)

    square = jnp.zeros((tokens, 1), F32)
    for c in range(chunks):
        for g in range(groups):
            piece_copy(c, g).wait()
        for lo in range(0, width, 256):
            acc = sum(jnp.dot(mix_ref[:, g * piece:(g + 1) * piece],
                              wbuf[2 * (c % 2) + g // 4, 0:piece, (g % 4) * width + lo:(g % 4) * width + lo + 256],
                              preferred_element_type=F32) for g in range(groups))
            x1 = (x_in[:, c * width + lo:c * width + lo + 256].astype(F32) + acc).astype(BF16)
            h_ref[c, :, lo:lo + 256] = x1
            x1 = x1.astype(F32)
            square += jnp.sum(x1 * x1, axis=-1, keepdims=True)
        if c + 2 < chunks:
            for g in range(groups):
                piece_copy(c + 2, g).start()
            if c == 1:
                weight(0).start()
        else:
            for i in (1, 2) if c % 2 == 0 else (3, 4):
                weight(i).start()
        push(2, c).start()
        push(4, c).start()
    inv = lax.rsqrt(square / d_model + NORM_EPS)
    meta_ref[2:3, :] = jnp.broadcast_to(inv, (tokens, tokens)).T[0:1]
    logits = jnp.zeros((tokens, n_experts), F32)
    for q in range(chunks):
        h2 = (h_ref[q].astype(F32) * inv * gain_ref[q * width:(q + 1) * width].astype(F32).reshape(1, -1)).astype(BF16)
        logits += lax.dot_general(h2, wr_ref[:, q * width:(q + 1) * width], (((1,), (1,)), ((), ())), preferred_element_type=F32)
    for r in (6, 2, 4, 7, 3, 5, 1):
        meta_copy(r).start()
    for q in range(chunks):
        push(1, q).start()
    lane = lax.broadcasted_iota(jnp.int32, logits.shape, 1).astype(F32) * cap
    own = [cols_ref[:, k:k + 1] for k in range(2)]
    p0, p1 = (jnp.sum(jnp.where((lane <= c) & (c < lane + cap), logits, 0.0), axis=-1, keepdims=True) for c in own)
    top = jnp.maximum(p0, p1)
    e0, e1 = jnp.exp(p0 - top), jnp.exp(p1 - top)
    gates_ref[:, 0:1] = e0 / (e0 + e1)
    gates_ref[:, 1:2] = e1 / (e0 + e1)

    slot_iota = lax.broadcasted_iota(jnp.int32, (local_experts * cap, tokens), 0)
    picks = {}

    def select(r, q):
        if r not in picks:
            if r:
                meta_copy(r).wait_recv()
            meta = meta_ref[...] if r == 0 else meta_in[r]
            want = (slot_iota + me * (local_experts * cap)).astype(F32)
            hit = (jnp.broadcast_to(meta[0:1], want.shape) == want) | (jnp.broadcast_to(meta[1:2], want.shape) == want)
            scale = jnp.sum(jnp.where(hit, jnp.broadcast_to(meta[2:3], want.shape), 0.0), axis=-1, keepdims=True)
            picks[r] = jnp.where(hit, 1.0, 0.0).astype(BF16), scale
        pick, scale = picks[r]
        got = jnp.dot(pick, block(r, q)[...], preferred_element_type=F32)
        got = (got * scale * gain_ref[q * width:(q + 1) * width].astype(F32).reshape(1, -1)).astype(BF16)
        for e in range(local_experts):
            x_ref[e, r * cap:(r + 1) * cap, q * width:(q + 1) * width] = got[e * cap:(e + 1) * cap]

    def y_copy(e, r):
        rows = pl.ds(r * cap, cap)
        return remote(x_ref.at[e, rows], y_in.at[e, rows], ysend.at[e, r], yrecv.at[e, r], r)

    def run_expert(e, lo_r, hi_r, slots, after_up=()):
        rows = slice(lo_r * cap, hi_r * cap)
        n_rows = (hi_r - lo_r) * cap
        for lo in range(0, d_ff, 256):
            hi = min(lo + 256, d_ff)
            gate, up = (lax.dot_general(x_ref[e, rows], wbuf[s, lo:hi], (((1,), (1,)), ((), ())), preferred_element_type=F32) for s in slots[:2])
            act_ref[0:n_rows, lo:hi] = (gate * jax.nn.sigmoid(gate) * up).astype(BF16)
        for i in after_up:
            weight(i).start()
        if e == 0 and lo_r == 0:
            weight(2).wait()
        if e == 1 and lo_r == 0:
            weight(5).wait()
        for lo in range(0, d_model, 512):
            x_ref[e, rows, lo:lo + 512] = jnp.dot(act_ref[0:n_rows], wbuf[slots[2], :, lo:lo + 512], preferred_element_type=F32).astype(BF16)

    for q in range(chunks):
        select(0, q)
    for q in range(chunks):
        for slot in (2, 4):
            push(slot, q).wait_recv()
            if (slot == 2) == (q < chunks // 2):
                push(6, q).start()
            push(slot + 1, q).start()
        for slot in (1, 2, 4):
            if slot == 1:
                push(slot, q).wait_recv()
            select(slot, q)
    for q in range(chunks):
        for slot in (3, 5):
            push(slot, q).wait_recv()
            select(slot, q)

    weight(0).wait()
    weight(1).wait()
    run_expert(0, 0, 6, (4, 0, 1), after_up=(5,))
    for r in (2, 4, 3, 5, 1):
        y_copy(0, r).start()
    y_in[0, 0:cap] = x_ref[0, 0:cap]
    weight(3).wait()
    weight(4).wait()
    run_expert(1, 0, 6, (2, 3, 4))
    for r in (2, 4, 3, 5, 1):
        y_copy(1, r).start()
    y_in[1, 0:cap] = x_ref[1, 0:cap]
    for q in (0, chunks // 2, 1, chunks // 2 + 1):
        push(6, q).wait_recv()
        push(7, q).start()
        select(6, q)
    for q in (0, chunks // 2, 1, chunks // 2 + 1):
        push(7, q).wait_recv()
        select(7, q)
    run_expert(1, 6, 8, (2, 3, 4), after_up=(6,))
    for r in (6, 7):
        y_copy(1, r).start()
    weight(6).wait()
    run_expert(0, 6, 8, (2, 0, 1))
    for r in (6, 7):
        y_copy(0, r).start()

    lane = lax.broadcasted_iota(jnp.int32, (tokens, rows_all), 1)
    rel, rank = lane // cap, lax.rem(lane, cap)
    owner = me + sum(lax.rem(rel // (1 << b), 2) * (1 << b) * (1 - 2 * bits[b]) for b in range(3))
    for e in (1, 0):
        for r in range(1, n_ep):
            y_copy(e, r).wait_recv()
        want = ((owner * local_experts + e) * cap + rank).astype(F32)
        sel = [jnp.where(cols_ref[:, k:k + 1] == want, 1.0, 0.0).astype(BF16) for k in range(2)]
        for lo in range(0, d_model, 512):
            y = y_in[e, :, lo:lo + 512]
            part = sum(gates_ref[:, k:k + 1] * jnp.dot(sel[k], y, preferred_element_type=F32) for k in range(2))
            if e:
                sum_ref[:, lo:lo + 512] = part
            else:
                x1 = h_ref[lo // width, :, lo % width:lo % width + 512].astype(F32)
                out_ref[:, lo:lo + 512] = (x1 + (sum_ref[:, lo:lo + 512] + part)).astype(BF16)

    for r in range(1, n_ep):
        meta_copy(r).wait_send()
        for q in range(chunks):
            push(r, q).wait_send()
        for e in range(local_experts):
            y_copy(e, r).wait_send()


def moe(hidden, mix, gain, w_router, expert_ids, w_out, w_gate, w_up, w_down, n_ep, cap):
    tokens, d_model = hidden.shape
    local_experts, d_ff, _ = w_down.shape
    vmem = pl.BlockSpec(memory_space=pltpu.VMEM)
    hbm = pl.BlockSpec(memory_space=pl.ANY)
    rows = n_ep * cap
    width = d_model // CHUNKS
    dma = pltpu.SemaphoreType.DMA
    return pl.pallas_call(
        functools.partial(moe_kernel, n_ep, n_ep * local_experts, cap),
        out_shape=jax.ShapeDtypeStruct((tokens, d_model), BF16),
        in_specs=[vmem] * 5 + [hbm] * 4,
        out_specs=vmem,
        scratch_shapes=[
            pltpu.VMEM((CHUNKS, tokens, width), BF16),
            pltpu.VMEM((n_ep - 1, CHUNKS, tokens, width), BF16),
            pltpu.VMEM((local_experts, rows, d_model), BF16),
            pltpu.VMEM((local_experts, rows, d_model), BF16),
            pltpu.VMEM((rows, d_ff), BF16),
            pltpu.VMEM((tokens, d_model), F32),
            pltpu.VMEM((tokens, 128), F32),
            pltpu.VMEM((tokens, 128), F32),
            pltpu.VMEM((8, tokens), F32),
            pltpu.VMEM((n_ep, 8, tokens), F32),
            pltpu.VMEM((5, d_ff, d_model), BF16),
            dma((16,)), dma((7,)), dma((n_ep,)), dma((n_ep,)), dma((n_ep, CHUNKS)), dma((n_ep, CHUNKS)),
            dma((local_experts, n_ep)), dma((local_experts, n_ep)),
        ],
        compiler_params=pltpu.CompilerParams(vmem_limit_bytes=67043328, collective_id=0, has_side_effects=True),
    )(hidden, mix, gain, w_router.T, expert_ids.T, w_out, jnp.swapaxes(w_gate, 1, 2), jnp.swapaxes(w_up, 1, 2), w_down)


def solution(mesh):
    n_ep = mesh.shape['ep']
    row_spec = P(('dp', 'ep'), None)
    cache_spec = P(('dp', 'ep'), None, None, None)
    expert_spec = P('ep', None, None)
    in_specs = (row_spec, cache_spec, cache_spec, P(('dp', 'ep')), row_spec, P(), P(), P(), P(), P(), P(), P(), expert_spec, expert_spec, expert_spec)
    out_specs = (row_spec, cache_spec, cache_spec)

    def device_step(hidden, k_cache, v_cache, seq_lens, expert_ids, attn_gain, w_query, w_key, w_value, w_out, ffn_gain, w_router, w_gate, w_up, w_down):
        tokens, d_model = hidden.shape
        local_experts = w_gate.shape[0]
        n_experts = local_experts * n_ep
        cap_slots = 4 * tokens // n_experts
        k_cache_new, v_cache_new, mix = attend(hidden, attn_gain, seq_lens, w_query, w_key, w_value, k_cache, v_cache)
        out = moe(hidden, mix, ffn_gain, w_router, expert_ids, w_out, w_gate, w_up, w_down, n_ep, cap_slots)
        return out, k_cache_new, v_cache_new

    return jax.shard_map(device_step, mesh=mesh, in_specs=in_specs, out_specs=out_specs, check_vma=False)
```

time: 165 us -> 128 us (0.78)
  Pallas kernels: 155 us -> 124 us
  local copies, waits for them, and re-layouts: 6.31 us -> 2.29 us
    pallas_call x4 -> x2, Pallas kernels: 155 us -> 124 us  [the longest x1 94.6 us: moe(): pl.pallas_call(functools.partial(moe_kernel, n_ep, n_ep * local_experts,...]
    reshape x2 -> x0, local copies, waits for them, and re-layouts: 1.92 us -> none  [the longest x1 1.31 us: qkv_project(): gain.reshape(1, -1)]
where the time goes in v3:
time: 128 us
  Pallas kernels  124 us (97%)
  local copies, waits for them, and re-layouts  2.29 us (2%)
    pallas_call x1, Pallas kernels, moe(): pl.pallas_call(functools.partial(moe_kernel, n_ep, n_ep * local_experts,...  94.6 us
    pallas_call x1, Pallas kernels, attend(): pl.pallas_call(attend_kernel, out_shape=[jax.ShapeDtypeStruct(k_cache.sha...  29.7 us

profile of v3, /device:TPU:0, one launch (start us, length us, event | category | flops | bytes accessed | tf_op | source)
XLA Modules:
  0.0 127.8 jit_solution(7343355071369145030)
XLA Ops:
  0.6 0.6 maximum_bitcast_fusion.freq_ref
  1.2 29.7 %shard_map.166 = (bf16[128,32,8,128]{3,2,1,0:T(8,128)(2,1)}, bf16[128,32,8,128]{3,2,1,0:T(8,128)(2,1)}, bf16[128,4096]{1,0:T(8,128)(2,1)}) custom-call(s32[128]{0:T(128)} %lens_ref.1, bf16[128,4096]{1,0:T(8,128)(2,1)} %x_in.1, bf16[4096]{0:T(1024)(128)(2,1)} %gain_ref.2, f32[1,128]{1,0:T(1,128)} %maximum_bitcast_fusion.freq_ref, bf16[4096,4096]{1,0:T(8,128)(2,1)} %wq.1, ...), custom_call_target="tpu_custom_call" | custom-call | tf_op jit(solution)/shard_map/pallas_call | solution.py:141
  30.9 94.6 %shard_map.167 = bf16[128,4096]{1,0:T(8,128)(2,1)} custom-call(bf16[128,4096]{1,0:T(8,128)(2,1)} %x_in.1, bf16[128,4096]{1,0:T(8,128)(2,1)} %get-tuple-element.6.mix_ref, bf16[4096]{0:T(1024)(128)(2,1)} %gain_ref.3, bf16[16,4096]{1,0:T(8,128)(2,1)} %bitcast.8, s32[2,128]{1,0:T(2,128)} %bitcast.9, bf16[4096,4096]{1,0:T(8,128)(2,1)} %wo.1, ...), custom_call_target="tpu_custom_call" | custom-call | tf_op jit(solution)/shard_map/pallas_call | solution.py:378
  125.5 2.3 %copy.19 = bf16[128,4096]{1,0:T(8,128)(2,1)} copy(bf16[128,4096]{1,0:T(8,128)(2,1)} %shard_map.167) | data formatting | bytes 2097152
  (1 shorter events, 0.0 us)

commit v4 on v3

--- a/solution.py
+++ b/solution.py
@@ -155,10 +155,12 @@
     )(positions, hidden, gain, freq, wq, wk, wv, k_cache, v_cache)
 
 
-def moe_kernel(n_ep, n_experts, cap, x_in, mix_ref, gain_ref, wr_ref, ids_ref, wo, wg, wu, wd, out_ref,
-               h_ref, buf, x_ref, y_in, act_ref, sum_ref, gates_ref, cols_ref, meta_ref, meta_in, wbuf,
-               osem, wsem, csend, crecv, gsend, grecv, ysend, yrecv):
+def moe_kernel(n_ep, n_dp, n_experts, cap, x_in, mix_ref, gain_ref, wr_ref, ids_ref, wo, wg, wu, wd, out_ref, gates_ref, cols_ref, flag_out, spill,
+               h_ref, buf, x_ref, y_first, y_rest, act_ref, meta_ref, meta_in, flag_ref, flag_in, wbuf,
+               osem, wsem, csend, crecv, gsend, grecv, ysend, yrecv, fsend, frecv, ssem):
     me = lax.axis_index('ep')
+    group = lax.axis_index('dp')
+    half = cap // 2
     bits = [lax.rem(me, 2), lax.rem(me // 2, 2), me // 4]
     chunks, tokens, width = h_ref.shape
     d_model = chunks * width
@@ -200,6 +202,10 @@
         m, e, slot = loads[i]
         return pltpu.make_async_copy((wg, wu, wd)[m].at[e], wbuf.at[slot], wsem.at[i])
 
+    def flag_copy(d):
+        return pltpu.make_async_remote_copy(src_ref=flag_ref, dst_ref=flag_in.at[d], send_sem=fsend.at[d], recv_sem=frecv.at[d],
+                                            device_id={'dp': lax.rem(group + d, n_dp)}, device_id_type=pl.DeviceIdType.MESH)
+
     def meta_copy(r):
         return remote(meta_ref, meta_in.at[r], csend.at[r], crecv.at[r], r)
 
@@ -209,16 +215,32 @@
     barrier = pltpu.get_barrier_semaphore()
     for r in range(1, n_ep):
         pl.semaphore_signal(barrier, inc=1, device_id={'ep': peer(r)}, device_id_type=pl.DeviceIdType.MESH)
+    for d in range(1, n_dp):
+        pl.semaphore_signal(barrier, inc=1, device_id={'dp': lax.rem(group + d, n_dp)}, device_id_type=pl.DeviceIdType.MESH)
 
     expert = lax.broadcasted_iota(jnp.int32, (n_experts, tokens), 0)
     hits = [jnp.where(jnp.broadcast_to(ids_ref[k:k + 1, :], expert.shape) == expert, 1.0, 0.0) for k in range(2)]
     earlier = lax.broadcasted_iota(jnp.int32, (tokens, tokens), 0) < lax.broadcasted_iota(jnp.int32, (tokens, tokens), 1)
     before = jnp.dot((hits[0] + hits[1]).astype(BF16), jnp.where(earlier, 1.0, 0.0).astype(BF16), preferred_element_type=F32)
     code = [ids_ref[k:k + 1, :].astype(F32) * cap + jnp.sum(hits[k] * before, axis=0, keepdims=True) for k in range(2)]
-    meta_ref[...] = jnp.concatenate([jnp.broadcast_to(c, (1, tokens)) for c in code] + [jnp.zeros((6, tokens), F32)], axis=0)
+    counts = jnp.broadcast_to(jnp.sum(hits[0] + hits[1], axis=1, keepdims=True), before.shape)
+    odd = lax.rem(expert, 2)
+    off_x, off_y = lax.rem(expert // 4, 2), expert // 8
+    off_x = off_x + bits[1] - 2 * off_x * bits[1]
+    off_y = off_y + bits[2] - 2 * off_y * bits[2]
+    first = lax.rem(odd + off_x * off_y, 2) == 0
+    other = jnp.where(odd == 0, pltpu.roll(counts, n_experts - 1, 0), pltpu.roll(counts, 1, 0))
+    device = (expert // 2).astype(F32)
+    later = jnp.where(first, before - half + other, before)
+    place = jnp.where(first & (before < half), device * half + before, n_ep * cap + device * (2 * cap) + later)
+    over = jnp.where(first & (before < half), 0.0, jnp.where(later >= cap, 1.0, 0.0))
+    places = [jnp.sum(hits[k] * place, axis=0, keepdims=True) for k in range(2)]
+    spilled = jnp.max(jnp.max((hits[0] + hits[1]) * over, axis=0, keepdims=True), axis=1, keepdims=True)
+    zero = jnp.zeros((1, tokens), F32)
+    meta_ref[...] = jnp.concatenate(code + [zero] + places + [zero + spilled, zero, zero], axis=0)
     cols_ref[...] = jnp.concatenate([meta_ref[...]] * (tokens // 8), axis=0).T
 
-    pl.semaphore_wait(barrier, n_ep - 1)
+    pl.semaphore_wait(barrier, n_ep + n_dp - 2)
 
     square = jnp.zeros((tokens, 1), F32)
     for c in range(chunks):
@@ -278,9 +300,33 @@
         for e in range(local_experts):
             x_ref[e, r * cap:(r + 1) * cap, q * width:(q + 1) * width] = got[e * cap:(e + 1) * cap]
 
-    def y_copy(e, r):
-        rows = pl.ds(r * cap, cap)
-        return remote(x_ref.at[e, rows], y_in.at[e, rows], ysend.at[e, r], yrecv.at[e, r], r)
+    def y_copy(p, r):
+        rows = pl.ds(r * cap, half if p == 0 else cap)
+        dst = y_first.at[pl.ds(r * half, half)] if p == 0 else y_rest.at[pl.ds(r * cap, cap)]
+        return remote(x_ref.at[p if r < 6 else 1 - p, rows], dst, ysend.at[p, r], yrecv.at[p, r], r)
+
+    def compact(r):
+        f = int(r >= 6)
+        meta = meta_ref[...] if r == 0 else meta_in[r]
+        lo = ((me * 2 + 1 - f) * cap).astype(F32)
+        mine = jnp.where((meta[0:2] >= lo) & (meta[0:2] < lo + cap), 1.0, 0.0)
+        n_odd = jnp.sum(jnp.sum(mine, axis=0, keepdims=True), axis=1, keepdims=True)
+        shape = (cap + half, 2 * cap)
+        to = lax.broadcasted_iota(jnp.int32, shape, 0).astype(F32)
+        frm = lax.broadcasted_iota(jnp.int32, shape, 1).astype(F32)
+        count = jnp.broadcast_to(n_odd, shape)
+        odd = (frm >= cap) & (frm - cap < count) & (to == frm - cap)
+        rest = (frm >= half) & (frm < cap) & (to == frm - half + count)
+        move = jnp.where(odd | rest, 1.0, 0.0).astype(BF16)
+        rows = slice(r * cap, (r + 1) * cap)
+        for lo in range(0, d_model, 512):
+            y = jnp.concatenate([x_ref[f, rows, lo:lo + 512], x_ref[1 - f, rows, lo:lo + 512]], axis=0)
+            z = jnp.dot(move, y, preferred_element_type=F32).astype(BF16)
+            x_ref[1 - f, rows, lo:lo + 512] = z[:cap]
+            x_ref[f, r * cap + half:(r + 1) * cap, lo:lo + 512] = z[cap:]
+
+    def spill_copy(r):
+        return pltpu.make_async_copy(x_ref.at[int(r >= 6), pl.ds(r * cap + half, half)], spill.at[peer(r)], ssem.at[r])
 
     def run_expert(e, lo_r, hi_r, slots, after_up=()):
         rows = slice(lo_r * cap, hi_r * cap)
@@ -320,13 +366,15 @@
     run_expert(0, 0, 6, (4, 0, 1), after_up=(5,))
     for r in (2, 4, 3, 5, 1):
         y_copy(0, r).start()
-    y_in[0, 0:cap] = x_ref[0, 0:cap]
+    y_first[0:half] = x_ref[0, 0:half]
     weight(3).wait()
     weight(4).wait()
     run_expert(1, 0, 6, (2, 3, 4))
     for r in (2, 4, 3, 5, 1):
+        compact(r)
         y_copy(1, r).start()
-    y_in[1, 0:cap] = x_ref[1, 0:cap]
+    compact(0)
+    y_rest[0:cap] = x_ref[1, 0:cap]
     for q in (0, chunks // 2, 1, chunks // 2 + 1):
         push(6, q).wait_recv()
         push(7, q).start()
@@ -336,29 +384,47 @@
         select(7, q)
     run_expert(1, 6, 8, (2, 3, 4), after_up=(6,))
     for r in (6, 7):
-        y_copy(1, r).start()
+        y_copy(0, r).start()
     weight(6).wait()
     run_expert(0, 6, 8, (2, 0, 1))
     for r in (6, 7):
-        y_copy(0, r).start()
-
-    lane = lax.broadcasted_iota(jnp.int32, (tokens, rows_all), 1)
-    rel, rank = lane // cap, lax.rem(lane, cap)
-    owner = me + sum(lax.rem(rel // (1 << b), 2) * (1 << b) * (1 - 2 * bits[b]) for b in range(3))
-    for e in (1, 0):
+        compact(r)
+        y_copy(1, r).start()
+    flag = meta_ref[5:6]
+    for r in range(1, n_ep):
+        flag = jnp.maximum(flag, meta_in[r, 5:6])
+    flag_ref[...] = jnp.broadcast_to(flag, flag_ref.shape)
+    for d in range(1, n_dp):
+        flag_copy(d).start()
+    for r in range(n_ep):
+        spill_copy(r).start()
+
+    for p, per, y_ref in ((0, half, y_first), (1, cap, y_rest)):
+        lane = lax.broadcasted_iota(jnp.int32, (tokens, n_ep * per), 1)
+        rel, rank = lane // per, lax.rem(lane, per)
+        owner = me + sum(lax.rem(rel // (1 << b), 2) * (1 << b) * (1 - 2 * bits[b]) for b in range(3))
+        want = (owner * half + rank if p == 0 else n_ep * cap + owner * (2 * cap) + rank).astype(F32)
+        sel = [jnp.where(cols_ref[:, 3 + k:4 + k] == want, 1.0, 0.0).astype(BF16) for k in range(2)]
         for r in range(1, n_ep):
-            y_copy(e, r).wait_recv()
-        want = ((owner * local_experts + e) * cap + rank).astype(F32)
-        sel = [jnp.where(cols_ref[:, k:k + 1] == want, 1.0, 0.0).astype(BF16) for k in range(2)]
+            y_copy(p, r).wait_recv()
         for lo in range(0, d_model, 512):
-            y = y_in[e, :, lo:lo + 512]
+            y = y_ref[:, lo:lo + 512]
             part = sum(gates_ref[:, k:k + 1] * jnp.dot(sel[k], y, preferred_element_type=F32) for k in range(2))
-            if e:
-                sum_ref[:, lo:lo + 512] = part
+            if p == 0:
+                out_ref[:, lo:lo + 512] = part
             else:
                 x1 = h_ref[lo // width, :, lo % width:lo % width + 512].astype(F32)
-                out_ref[:, lo:lo + 512] = (x1 + (sum_ref[:, lo:lo + 512] + part)).astype(BF16)
-
+                out_ref[:, lo:lo + 512] = x1 + (out_ref[:, lo:lo + 512] + part)
+
+    flag = flag_ref[...]
+    for d in range(1, n_dp):
+        flag_copy(d).wait_recv()
+        flag = jnp.maximum(flag, flag_in[d])
+    flag_out[...] = flag
+    for d in range(1, n_dp):
+        flag_copy(d).wait_send()
+    for r in range(n_ep):
+        spill_copy(r).wait()
     for r in range(1, n_ep):
         meta_copy(r).wait_send()
         for q in range(chunks):
@@ -367,36 +433,49 @@
             y_copy(e, r).wait_send()
 
 
-def moe(hidden, mix, gain, w_router, expert_ids, w_out, w_gate, w_up, w_down, n_ep, cap):
+def moe(hidden, mix, gain, w_router, expert_ids, w_out, w_gate, w_up, w_down, n_ep, n_dp, cap):
     tokens, d_model = hidden.shape
     local_experts, d_ff, _ = w_down.shape
+    half = cap // 2
     vmem = pl.BlockSpec(memory_space=pltpu.VMEM)
     hbm = pl.BlockSpec(memory_space=pl.ANY)
     rows = n_ep * cap
     width = d_model // CHUNKS
     dma = pltpu.SemaphoreType.DMA
-    return pl.pallas_call(
-        functools.partial(moe_kernel, n_ep, n_ep * local_experts, cap),
-        out_shape=jax.ShapeDtypeStruct((tokens, d_model), BF16),
+    total, gates, cols, flag, spill = pl.pallas_call(
+        functools.partial(moe_kernel, n_ep, n_dp, n_ep * local_experts, cap),
+        out_shape=[jax.ShapeDtypeStruct((tokens, d_model), F32), jax.ShapeDtypeStruct((tokens, 128), F32), jax.ShapeDtypeStruct((tokens, 128), F32),
+                   jax.ShapeDtypeStruct((8, tokens), F32), jax.ShapeDtypeStruct((n_ep, half, d_model), BF16)],
         in_specs=[vmem] * 5 + [hbm] * 4,
-        out_specs=vmem,
+        out_specs=[vmem] * 4 + [hbm],
         scratch_shapes=[
             pltpu.VMEM((CHUNKS, tokens, width), BF16),
             pltpu.VMEM((n_ep - 1, CHUNKS, tokens, width), BF16),
             pltpu.VMEM((local_experts, rows, d_model), BF16),
-            pltpu.VMEM((local_experts, rows, d_model), BF16),
+            pltpu.VMEM((n_ep * half, d_model), BF16),
+            pltpu.VMEM((n_ep * cap, d_model), BF16),
             pltpu.VMEM((rows, d_ff), BF16),
-            pltpu.VMEM((tokens, d_model), F32),
-            pltpu.VMEM((tokens, 128), F32),
-            pltpu.VMEM((tokens, 128), F32),
             pltpu.VMEM((8, tokens), F32),
             pltpu.VMEM((n_ep, 8, tokens), F32),
+            pltpu.VMEM((8, tokens), F32),
+            pltpu.VMEM((n_dp, 8, tokens), F32),
             pltpu.VMEM((5, d_ff, d_model), BF16),
             dma((16,)), dma((7,)), dma((n_ep,)), dma((n_ep,)), dma((n_ep, CHUNKS)), dma((n_ep, CHUNKS)),
-            dma((local_experts, n_ep)), dma((local_experts, n_ep)),
+            dma((2, n_ep)), dma((2, n_ep)), dma((n_dp,)), dma((n_dp,)), dma((n_ep,)),
         ],
         compiler_params=pltpu.CompilerParams(vmem_limit_bytes=67043328, collective_id=0, has_side_effects=True),
     )(hidden, mix, gain, w_router.T, expert_ids.T, w_out, jnp.swapaxes(w_gate, 1, 2), jnp.swapaxes(w_up, 1, 2), w_down)
+
+    def with_spill(total, gates, cols, spill):
+        rows_in = lax.all_to_all(spill, 'ep', 0, 0, tiled=True).reshape(n_ep * half, d_model)
+        at = jnp.arange(n_ep * half)
+        want = (n_ep * cap + at // half * (2 * cap) + cap + at % half).astype(F32)
+        for k in range(2):
+            sel = (cols[:, 3 + k:4 + k] == want).astype(BF16)
+            total = total + gates[:, k:k + 1] * jnp.dot(sel, rows_in, preferred_element_type=F32)
+        return total.astype(BF16)
+
+    return lax.cond(flag[0, 0] > 0, with_spill, lambda total, gates, cols, spill: total.astype(BF16), total, gates, cols, spill)
 
 
 def solution(mesh):
@@ -413,7 +492,7 @@
         n_experts = local_experts * n_ep
         cap_slots = 4 * tokens // n_experts
         k_cache_new, v_cache_new, mix = attend(hidden, attn_gain, seq_lens, w_query, w_key, w_value, k_cache, v_cache)
-        out = moe(hidden, mix, ffn_gain, w_router, expert_ids, w_out, w_gate, w_up, w_down, n_ep, cap_slots)
+        out = moe(hidden, mix, ffn_gain, w_router, expert_ids, w_out, w_gate, w_up, w_down, n_ep, mesh.shape['dp'], cap_slots)
         return out, k_cache_new, v_cache_new
 
     return jax.shard_map(device_step, mesh=mesh, in_specs=in_specs, out_specs=out_specs, check_vma=False)

time: 128 us -> 122 us (0.953)
  Pallas kernels: 124 us -> 115 us
  other arithmetic: 0.59 us -> 3.36 us
    pallas_call x1, Pallas kernels: 94.6 us -> 85.2 us  [moe(): pl.pallas_call(functools.partial(moe_kernel, n_ep, n_dp, n_ep * local_exp...]
    convert_element_type x0 -> x1, other arithmetic: none -> 2.69 us  [moe(): total.astype(BF16)]
    unnamed x1 -> x0, local copies, waits for them, and re-layouts: 2.29 us -> none
where the time goes in v4:
time: 122 us; the launch traced here: 121 us
  Pallas kernels  115 us (94%)
  other arithmetic  3.36 us (3%)
  between operations  1.3 us (1%)
    pallas_call x1, Pallas kernels, moe(): pl.pallas_call(functools.partial(moe_kernel, n_ep, n_dp, n_ep * local_exp...  85.2 us
    pallas_call x1, Pallas kernels, attend(): pl.pallas_call(attend_kernel, out_shape=[jax.ShapeDtypeStruct(k_cache.sha...  29.7 us
    convert_element_type x1, other arithmetic, moe(): total.astype(BF16)  2.69 us

profile of v4, /device:TPU:0, one launch (start us, length us, event | category | flops | bytes accessed | tf_op | source)
XLA Modules:
  0.0 120.8 jit_solution(798640720063873502)
XLA Ops:
  0.6 0.7 maximum_bitcast_fusion.freq_ref
  1.3 29.7 %shard_map.166 = (bf16[128,32,8,128]{3,2,1,0:T(8,128)(2,1)}, bf16[128,32,8,128]{3,2,1,0:T(8,128)(2,1)}, bf16[128,4096]{1,0:T(8,128)(2,1)}) custom-call(s32[128]{0:T(128)} %lens_ref.1, bf16[128,4096]{1,0:T(8,128)(2,1)} %x_in.1, bf16[4096]{0:T(1024)(128)(2,1)} %gain_ref.2, f32[1,128]{1,0:T(1,128)} %maximum_bitcast_fusion.freq_ref, bf16[4096,4096]{1,0:T(8,128)(2,1)} %wq.1, ...), custom_call_target="tpu_custom_call" | custom-call | tf_op jit(solution)/shard_map/pallas_call | solution.py:141
  31.0 85.2 %shard_map.167 = (f32[128,4096]{1,0:T(8,128)}, f32[128,128]{1,0:T(8,128)}, f32[128,128]{1,0:T(8,128)}, f32[8,128]{1,0:T(8,128)}, bf16[8,16,4096]{2,1,0:T(8,128)(2,1)}) custom-call(bf16[128,4096]{1,0:T(8,128)(2,1)} %x_in.1, bf16[128,4096]{1,0:T(8,128)(2,1)} %get-tuple-element.33.mix_ref, bf16[4096]{0:T(1024)(128)(2,1)} %gain_ref.3, ...), custom_call_target="tpu_custom_call" | custom-call | tf_op jit(solution)/shard_map/pallas_call | solution.py:445
  116.2 1.2 slice.15
  118.1 2.7 %conditional.1 = (bf16[128,4096]{1,0:T(8,128)(2,1)}) conditional(s32[]{:T(128)} %bitcast.10, f32[128,4096]{1,0:T(8,128)} %get-tuple-element.35, (f32[128,128]{1,0:T(8,128)}, f32[128,128]{1,0:T(8,128)}, bf16[8,16,4096]{2,1,0:T(8,128)(2,1)}, f32[128,4096]{1,0:T(8,128)}) %tuple.24), branch_computations={%region_0.0_spmd, %region_1.2_spmd} | conditional | flops 271091712 | bytes 21503584 | solution.py:478
  118.1 2.7 %convert_element_type.23 = bf16[128,4096]{1,0:T(8,128)(2,1)} convert(f32[128,4096]{1,0:T(8,128)} %param) | non-fusion elementwise | flops 524288 | bytes 3145728 | tf_op jit(solution)/shard_map/cond/branch_0_fun/convert_element_type | solution.py:478
  (1 shorter events, 0.0 us)
